TPU v7x, 8 devices: a whole 2x2x1 slice. The times are simulated.
8 devices in a mesh: dp: 1 (over z), col: 2 (over y), row: 4 (over x, core).
Axes of the slice: x: 2, y: 2, z: 1, core: 2. Of those that a mesh axis runs over, the one named last changes fastest.
Arguments:
- x_in: bfloat16 [2048, 2048], P(('dp', 'row'), 'col')
- w_qkv: bfloat16 [2048, 6144], P('row', 'col')
- w_out: bfloat16 [2048, 2048], P('row', 'col')
- doc_ids: int32 [2048], P(('dp', 'row'))
- grad_y: bfloat16 [2048, 2048], P(('dp', 'row'), 'col')
Outputs:
- output 1: bfloat16 [2048, 2048], P(('dp', 'row'), 'col')
- output 2: bfloat16 [2048, 6144], P(('dp', 'row'), 'col')
- output 3: bfloat16 [2048, 2048], P(('dp', 'row'), 'col')
All inputs are finite; a program needn't handle non-finite values.
Results may differ from a plain program's by a relative error of at most 0.00385.
Values are sent between devices in bfloat16 or wider.
A program may use at most 1 GiB of HBM per device.

v0:
```python
import jax
import jax.numpy as jnp
from jax import lax
from jax.sharding import PartitionSpec as P

HEAD_DIM = 128


def solution(mesh):
    tok_spec = P(('dp', 'row'), 'col')
    mat_spec = P('row', 'col')
    seg_spec = P(('dp', 'row'))
    contract_last = (((1,), (1,)), ((), ()))
    contract_first = (((0,), (0,)), ((), ()))

    def grad_step(x_blk, wqkv_blk, wout_blk, seg_blk, dy_blk):
        seq_loc, width_loc = x_blk.shape
        n_loc = width_loc // HEAD_DIM
        sm_scale = HEAD_DIM ** -0.5
        x_row = lax.all_gather(x_blk, 'col', axis=1, tiled=True)
        w_col = lax.all_gather(wqkv_blk, 'row', axis=0, tiled=True)
        qkv_loc = jnp.dot(x_row, w_col, preferred_element_type=jnp.float32).astype(jnp.bfloat16)
        qkv_loc = qkv_loc.reshape(seq_loc, n_loc, 3, HEAD_DIM)
        q_loc = qkv_loc[:, :, 0]
        kv_all = lax.all_gather(qkv_loc[:, :, 1:], 'row', axis=0, tiled=True)
        k_all = kv_all[:, :, 0]
        v_all = kv_all[:, :, 1]
        seg_all = lax.all_gather(seg_blk, 'row', axis=0, tiled=True)
        wout_col = lax.all_gather(wout_blk, 'row', axis=0, tiled=True)
        do_part = lax.dot_general(dy_blk, wout_col, contract_last, preferred_element_type=jnp.float32)
        d_attn = lax.psum_scatter(do_part, 'col', scatter_dimension=1, tiled=True)
        d_attn = d_attn.astype(jnp.bfloat16).reshape(seq_loc, n_loc, HEAD_DIM)
        same_doc = seg_blk[:, None] == seg_all[None, :]
        scores = jnp.einsum('qhd,khd->hqk', q_loc, k_all, preferred_element_type=jnp.float32) * sm_scale
        scores = jnp.where(same_doc[None], scores, -jnp.inf)
        p_attn = jax.nn.softmax(scores, axis=-1)
        p_bf = p_attn.astype(jnp.bfloat16)
        attn_out = jnp.einsum('hqk,khd->qhd', p_bf, v_all, preferred_element_type=jnp.float32)
        attn_out = attn_out.astype(jnp.bfloat16).reshape(seq_loc, width_loc)
        d_probs = jnp.einsum('qhd,khd->hqk', d_attn, v_all, preferred_element_type=jnp.float32)
        row_dot = jnp.sum(p_attn * d_probs, axis=-1, keepdims=True)
        d_scores = (p_attn * (d_probs - row_dot) * sm_scale).astype(jnp.bfloat16)
        dq_loc = jnp.einsum('hqk,khd->qhd', d_scores, k_all, preferred_element_type=jnp.float32)
        dk_part = jnp.einsum('hqk,qhd->khd', d_scores, q_loc, preferred_element_type=jnp.float32)
        dv_part = jnp.einsum('hqk,qhd->khd', p_bf, d_attn, preferred_element_type=jnp.float32)
        dkv_loc = lax.psum_scatter(jnp.stack([dk_part, dv_part], axis=2), 'row', scatter_dimension=0, tiled=True)
        d_qkv = jnp.concatenate([dq_loc[:, :, None], dkv_loc], axis=2)
        d_qkv = d_qkv.astype(jnp.bfloat16).reshape(seq_loc, 3 * width_loc)
        dx_part = lax.dot_general(d_qkv, w_col, contract_last, preferred_element_type=jnp.float32)
        grad_x = lax.psum_scatter(dx_part, 'col', scatter_dimension=1, tiled=True).astype(jnp.bfloat16)
        dw_part = lax.dot_general(x_row, d_qkv, contract_first, preferred_element_type=jnp.float32)
        grad_wqkv = lax.psum_scatter(dw_part, 'row', scatter_dimension=0, tiled=True).astype(jnp.bfloat16)
        attn_row = lax.all_gather(attn_out, 'col', axis=1, tiled=True)
        dwo_part = lax.dot_general(attn_row, dy_blk, contract_first, preferred_element_type=jnp.float32)
        grad_wout = lax.psum_scatter(dwo_part, 'row', scatter_dimension=0, tiled=True).astype(jnp.bfloat16)
        return grad_x, grad_wqkv, grad_wout

    return jax.shard_map(grad_step, mesh=mesh, in_specs=(tok_spec, mat_spec, mat_spec, seg_spec, tok_spec), out_specs=(tok_spec, tok_spec, tok_spec), check_vma=False)
```

profile of v0, /device:TPU:0, one launch (start us, length us, event | category | flops | bytes accessed | tf_op | source)
XLA Modules:
  0.0 860.1 jit_solution(996508062486101323)
XLA Ops:
  7.2 0.7 all-gather.13.cloned.1.call-update
  7.9 0.0 all-gather.7.cloned.1.call-start
  8.0 0.7 all-gather.7.cloned.1.call-update
  8.7 0.7 all-gather.9.cloned.1.call-update
  9.4 0.0 reduce-scatter.6.cloned.1.call-start
  9.4 34.4 %all-gather.13.cloned.1.call-done = bf16[2048,1024]{1,0:T(8,128)(2,1)} async-done(((bf16[512,1024]{1,0:T(8,128)(2,1)}), bf16[2048,1024]{1,0:T(8,128)(2,1)}) %all-gather.13.cloned.1.call-update) | async-done | bytes 4194320 | tf_op jit(solution)/shard_map/all_gather | solution.py:29
  43.9 6.5 fusion.43
  50.4 0.0 all-gather.11.cloned.1.call-start
  50.5 25.1 %all-gather.7.cloned.1.call-done = bf16[512,2048]{1,0:T(8,128)(2,1)} async-done(((bf16[512,1024]{1,0:T(8,128)(2,1)}), bf16[512,2048]{1,0:T(8,128)(2,1)}) %all-gather.7.cloned.1.call-update) | async-done | bytes 2097168 | tf_op jit(solution)/shard_map/all_gather | solution.py:20
  75.6 81.5 %all-gather.9.cloned.1.call-done = bf16[2048,3072]{1,0:T(8,128)(2,1)} async-done(((bf16[512,3072]{1,0:T(8,128)(2,1)}), bf16[2048,3072]{1,0:T(8,128)(2,1)}) %all-gather.9.cloned.1.call-update) | async-done | bytes 12582928 | tf_op jit(solution)/shard_map/all_gather | solution.py:21
  157.1 12.9 %convolution_convert_fusion = bf16[512,3072]{1,0:T(8,128)(2,1)} fusion(bf16[512,2048]{1,0:T(8,128)(2,1)} %all-gather.7.cloned.1.call-done, bf16[2048,3072]{1,0:T(8,128)(2,1)} %all-gather.9.cloned.1.call-done), kind=kOutput, calls=%fused_computation.20 | convolution fusion | flops 6444023808 | bytes 17825792 | tf_op jit(solution)/shard_map/dot_general | solution.py:22
  170.0 4.7 copy.26
  174.7 1.8 slice.16
  176.5 2.4 copy.39
  178.9 0.0 all-gather.15.cloned.1.call-start
  178.9 7.0 all-gather
  185.9 1.6 broadcast_compare_fusion
  187.5 23.2 %reduce-scatter.6.cloned.1.call-done = f32[512,1024]{1,0:T(8,128)} async-done(((f32[512,2048]{1,0:T(8,128)}), f32[512,1024]{1,0:T(8,128)}) %reduce-scatter.6.cloned.1.call-update) | async-done | bytes 2097168 | tf_op jit(solution)/shard_map/reduce_scatter | solution.py:31
  210.7 1.7 convert_element_type.33
  212.5 0.5 copy.41
  213.0 55.4 %all-gather.11.cloned.1.call-done = bf16[2048,8,2,128]{3,0,1,2:T(8,128)(2,1)} async-done(((bf16[512,8,2,128]{3,0,1,2:T(8,128)(2,1)}), bf16[2048,8,2,128]{3,0,1,2:T(8,128)(2,1)}) %all-gather.11.cloned.1.call-update) | async-done | bytes 8388624 | tf_op jit(solution)/shard_map/all_gather | solution.py:25
  268.4 18.1 %fusion.25 = f32[8,512,2048]{2,1,0:T(8,128)} fusion(bf16[2048,8,2,128]{3,0,1,2:T(8,128)(2,1)} %all-gather.11.cloned.1.call-done, bf16[512,8,3,128]{0,3,2,1:T(8,128)(2,1)} %bitcast.55), kind=kOutput, calls=%fused_computation.25 | convolution fusion | flops 2147483648 | bytes 38797312 | tf_op jit(solution)/shard_map/qhd,khd->hqk/dot_general | solution.py:34
  286.6 37.5 %fusion.42 = (f32[8,512]{1,0:T(8,128)S(1)}, f32[8,512,2048]{2,1,0:T(8,128)}) fusion(f32[8,512,2048]{2,1,0:T(8,128)} %fusion.25, pred[512,2048]{1,0:T(8,128)(4,1)S(1)} %copy-done.2), kind=kOutput, calls=%fused_computation.39 | output fusion | flops 50333696 | bytes 68173824 | tf_op jit(solution)/shard_map/sub | solution.py:36
  324.1 15.4 %fusion.19 = f32[2048,8,1,128]{0,3,1,2:T(8,128)} fusion(bf16[512,8,128]{0,2,1:T(8,128)(2,1)S(1)} %bitcast.57, f32[8,512,2048]{2,1,0:T(8,128)} %get-tuple-element.13, f32[8,512]{1,0:T(8,128)S(1)} %get-tuple-element.12), kind=kOutput, calls=%fused_computation.21 | convolution fusion | flops 2164260864 | bytes 43008000 | tf_op jit(solution)/shard_map/hqk,qhd->khd/dot_general | solution.py:45
  339.5 16.0 %fusion.27 = bf16[8,128,512]{2,1,0:T(8,128)(2,1)} fusion(bf16[2048,8,2,128]{3,0,1,2:T(8,128)(2,1)} %all-gather.11.cloned.1.call-done, f32[8,512,2048]{2,1,0:T(8,128)} %get-tuple-element.13, f32[8,512]{1,0:T(8,128)S(1)} %get-tuple-element.12), kind=kOutput, calls=%fused_computation.29 | convolution fusion | flops 2164785152 | bytes 38813696 | tf_op jit(solution)/shard_map/hqk,khd->qhd/dot_general | solution.py:38
  355.5 0.0 reduce-scatter.8.cloned.1.call-start
  355.6 15.3 %fusion.26 = f32[8,512,2048]{2,1,0:T(8,128)} fusion(bf16[512,8,128]{0,2,1:T(8,128)(2,1)S(1)} %bitcast.58, bf16[2048,8,2,128]{3,0,1,2:T(8,128)(2,1)} %all-gather.11.cloned.1.call-done), kind=kOutput, calls=%fused_computation.26 | convolution fusion | flops 2147483648 | bytes 38797312 | tf_op jit(solution)/shard_map/qhd,khd->hqk/dot_general | solution.py:40
  370.9 48.7 %fusion.22 = f32[2048,8,1,128]{0,3,1,2:T(8,128)} fusion(f32[8,512,2048]{2,1,0:T(8,128)} %fusion.26, bf16[512,8,3,128]{0,3,2,1:T(8,128)(2,1)} %bitcast.56, f32[8,512,2048]{2,1,0:T(8,128)} %get-tuple-element.13, f32[8,512]{1,0:T(8,128)S(1)} %get-tuple-element.12), kind=kOutput, calls=%fused_computation.22 | convolution fusion | flops 2206210048 | bytes 143687680 | tf_op jit(solution)/shard_map/hqk,qhd->khd/dot_general | solution.py:44
  419.6 11.7 %pad_maximum_fusion = f32[2048,8,2,128]{0,3,1,2:T(8,128)} fusion(f32[2048,8,1,128]{0,3,1,2:T(8,128)} %fusion.19, f32[2048,8,1,128]{0,3,1,2:T(8,128)} %fusion.22), kind=kLoop, calls=%fused_computation.8 | loop fusion | flops 4194304 | bytes 33554432 | tf_op jit(solution)/shard_map/stack | solution.py:46
  431.4 0.0 reduce-scatter.14.cloned.1.call-start
  431.4 7.2 fusion.45
  438.6 0.0 reduce-scatter.10.cloned.1.call-start
  438.7 46.1 %fusion.33 = bf16[512,8,1,128]{0,3,1,2:T(8,128)(2,1)S(1)} fusion(f32[8,512,2048]{2,1,0:T(8,128)} %fusion.26, bf16[2048,8,2,128]{3,0,1,2:T(8,128)(2,1)} %all-gather.11.cloned.1.call-done, f32[8,512,2048]{2,1,0:T(8,128)} %get-tuple-element.13, f32[8,512]{1,0:T(8,128)S(1)} %get-tuple-element.12), kind=kOutput, calls=%fused_computation.31 | convolution fusion | flops 2206734336 | bytes 139493376 | tf_op jit(solution)/shard_map/hqk,khd->qhd/dot_general | solution.py:43
  484.8 65.5 %reduce-scatter.8.cloned.1.call-done = f32[512,8,2,128]{0,3,1,2:T(8,128)} async-done(((f32[2048,8,2,128]{0,3,1,2:T(8,128)}), f32[512,8,2,128]{0,3,1,2:T(8,128)}) %reduce-scatter.8.cloned.1.call-update) | async-done | bytes 4194320 | tf_op jit(solution)/shard_map/reduce_scatter | solution.py:46
  550.3 2.5 convert.9
  552.8 0.3 pad_maximum_fusion.1
  553.0 0.3 copy.33
  553.4 1.7 copy-done.1
  555.0 11.3 %fusion.44 = f32[512,2048]{1,0:T(8,128)} fusion(bf16[512,3072]{0,1:T(8,128)(2,1)S(1)} %bitcast.59, bf16[2048,3072]{1,0:T(8,128)(2,1)} %all-gather.9.cloned.1.call-done), kind=kOutput, calls=%fused_computation.41 | convolution fusion | flops 6442450944 | bytes 19922944 | tf_op jit(solution)/shard_map/dot_general | solution.py:49
  566.3 0.0 reduce-scatter.12.cloned.1.call-start
  566.4 13.6 %convolution_bitcast_fusion = f32[2048,3072]{0,1:T(8,128)} fusion(bf16[512,3072]{0,1:T(8,128)(2,1)} %bitcast.60, bf16[512,2048]{1,0:T(8,128)(2,1)S(1)} %copy-done.4), kind=kOutput, calls=%fused_computation.13 | convolution fusion | flops 6442450944 | bytes 30408704 | tf_op jit(solution)/shard_map/dot_general | solution.py:51
  580.0 38.0 %reduce-scatter.14.cloned.1.call-done = f32[512,1024]{1,0:T(8,128)} async-done(((f32[2048,1024]{1,0:T(8,128)}), f32[512,1024]{1,0:T(8,128)}) %reduce-scatter.14.cloned.1.call-update) | async-done | bytes 2097168 | tf_op jit(solution)/shard_map/reduce_scatter | solution.py:55
  618.0 2.7 convert_element_type.41
  620.7 51.1 %reduce-scatter.10.cloned.1.call-done = f32[512,1024]{1,0:T(8,128)} async-done(((f32[512,2048]{1,0:T(8,128)}), f32[512,1024]{1,0:T(8,128)}) %reduce-scatter.10.cloned.1.call-update) | async-done | bytes 2097168 | tf_op jit(solution)/shard_map/reduce_scatter | solution.py:50
  671.8 2.7 convert_element_type.37
  674.5 168.8 %reduce-scatter.12.cloned.1.call-done = f32[512,3072]{0,1:T(8,128)} async-done(((f32[2048,3072]{0,1:T(8,128)}), f32[512,3072]{0,1:T(8,128)}) %reduce-scatter.12.cloned.1.call-update) | async-done | bytes 6291472 | tf_op jit(solution)/shard_map/reduce_scatter | solution.py:52
  843.3 4.8 convert_element_type.38
  848.1 4.6 copy.35
  (19 shorter events, 0.2 us)
Async XLA Ops:
  7.2 36.7 %copy-start = (bf16[512,1024]{1,0:T(8,128)(2,1)S(1)}, bf16[512,1024]{1,0:T(8,128)(2,1)}, u32[]{:S(2)}) copy-start(bf16[512,1024]{1,0:T(8,128)(2,1)} %param.9) | copy-start | bytes 3145732
  7.2 36.7 %all-gather.13.cloned.1.call-start = ((), (), s32[]{:S(2)}) async-start(), calls=%async_computation.8 | async-start | bytes 5242880 | tf_op jit(solution)/shard_map/all_gather | solution.py:29
  7.9 67.7 %all-gather.7.cloned.1.call-start = ((), (), s32[]{:S(2)}) async-start(), calls=%async_computation.5 | async-start | bytes 3145728 | tf_op jit(solution)/shard_map/all_gather | solution.py:20
  8.7 148.4 %all-gather.9.cloned.1.call-start = ((), (), s32[]{:S(2)}) async-start(), calls=%async_computation.6 | async-start | bytes 15728640 | tf_op jit(solution)/shard_map/all_gather | solution.py:21
  9.4 201.3 %reduce-scatter.6.cloned.1.call-start = ((), (), s32[]{:S(2)}) async-start(), calls=%async_computation.9 | async-start | bytes 6291456 | tf_op jit(solution)/shard_map/reduce_scatter | solution.py:31
  50.4 218.0 %all-gather.11.cloned.1.call-start = ((), (), s32[]{:S(2)}) async-start(), calls=%async_computation.7 | async-start | bytes 10485760 | tf_op jit(solution)/shard_map/all_gather | solution.py:25
  170.0 8.9 %copy-start.3 = (s32[512]{0:T(512)S(1)}, s32[512]{0:T(512)}, u32[]{:S(2)}) copy-start(s32[512]{0:T(512)} %param.8) | copy-start | bytes 6148
  178.9 252.6 %all-gather.15.cloned.1.call-start = ((), (), s32[]{:S(2)}) async-start(), calls=%async_computation.13 | async-start | bytes 3145728 | tf_op jit(solution)/shard_map/all_gather | solution.py:53
  213.0 73.6 %copy-start.2 = (pred[512,2048]{1,0:T(8,128)(4,1)S(1)}, pred[512,2048]{1,0:T(8,128)(4,1)}, u32[]{:S(2)}) copy-start(pred[512,2048]{1,0:T(8,128)(4,1)} %broadcast_compare_fusion) | copy-start | bytes 3145732
  355.5 194.8 %reduce-scatter.8.cloned.1.call-start = ((), (), s32[]{:S(2)}) async-start(), calls=%async_computation.10 | async-start | bytes 20971520 | tf_op jit(solution)/shard_map/reduce_scatter | solution.py:46
  431.4 186.6 %reduce-scatter.14.cloned.1.call-start = ((), (), s32[]{:S(2)}) async-start(), calls=%async_computation.14 | async-start | bytes 10485760 | tf_op jit(solution)/shard_map/reduce_scatter | solution.py:55
  438.6 233.2 %reduce-scatter.10.cloned.1.call-start = ((), (), s32[]{:S(2)}) async-start(), calls=%async_computation.11 | async-start | bytes 6291456 | tf_op jit(solution)/shard_map/reduce_scatter | solution.py:50
  553.3 1.7 copy-start.1
  555.0 11.4 %copy-start.4 = (bf16[512,2048]{1,0:T(8,128)(2,1)S(1)}, bf16[512,2048]{1,0:T(8,128)(2,1)}, u32[]{:S(2)}) copy-start(bf16[512,2048]{1,0:T(8,128)(2,1)} %all-gather.7.cloned.1.call-done) | copy-start | bytes 6291460
  566.3 277.0 %reduce-scatter.12.cloned.1.call-start = ((), (), s32[]{:S(2)}) async-start(), calls=%async_computation.12 | async-start | bytes 31457280 | tf_op jit(solution)/shard_map/reduce_scatter | solution.py:52
Sparse Core Ops, SparseCore 0:
  9.5 34.3 all-gather.12
  45.4 30.1 all-gather.6
  77.1 79.9 all-gather.8
  159.2 51.4 reduce-scatter.5
  212.7 55.7 all-gather.10
  355.6 30.1 all-gather.14
  431.5 118.7 reduce-scatter.7
  552.8 65.1 reduce-scatter.13
  620.2 51.5 reduce-scatter.9
  674.2 169.0 reduce-scatter.11
where the time goes:
time: 865 us; the launch traced here: 860 us
  waiting for transfers between devices  545 us (63%)
  matrix products  211 us (24%)
  other arithmetic  65.6 us (8%)
  local copies, waits for them, and re-layouts  16 us (2%)
  between operations  14.7 us (2%)
    reduce_scatter x1, waiting for transfers between devices, grad_step(): lax.psum_scatter(dw_part, 'row', scatter_dimension=0, tiled=True)  169 us
    all_gather x1, waiting for transfers between devices, grad_step(): w_col = lax.all_gather(wqkv_blk, 'row', axis=0, tiled=True)  81.5 us
    reduce_scatter x1, waiting for transfers between devices, grad_step(): lax.psum_scatter(jnp.stack([dk_part, dv_part], axis=2), 'row', scatter_di...  65.5 us
    all_gather x1, waiting for transfers between devices, grad_step(): kv_all = lax.all_gather(qkv_loc[:, :, 1:], 'row', axis=0, tiled=True)  55.4 us
    reduce_scatter x1, waiting for transfers between devices, grad_step(): lax.psum_scatter(dx_part, 'col', scatter_dimension=1, tiled=True)  51.1 us
    dot_general x1, matrix products, grad_step(): jnp.einsum('hqk,qhd->khd', d_scores, q_loc, preferred_element_type=jnp.fl...  48.7 us
    dot_general x1, matrix products, grad_step(): jnp.einsum('hqk,khd->qhd', d_scores, k_all, preferred_element_type=jnp.fl...  46.1 us
    reduce_scatter x1, waiting for transfers between devices, grad_step(): lax.psum_scatter(dwo_part, 'row', scatter_dimension=0, tiled=True)  38 us
  transfers between devices with their start and end apart: 10, of which 9 were waited for; matrix products, arithmetic and copies ran while one was open for 23% of the time, Pallas kernels for 0%

commit v1 on v0

v1 whole, which is shorter than its diff:
```python
import jax
import jax.numpy as jnp
from jax import lax
from jax.experimental import pallas as pl
from jax.experimental.pallas import tpu as pltpu
from jax.sharding import PartitionSpec as P

NT = (((1,), (1,)), ((), ()))
TN = (((0,), (0,)), ((), ()))
BQ = 256
BK = 512
D = 128

def attn_kernel(seg_ref, qkv_ref, do_ref, dqkv_ref, o_ref, cut, s_scr, dp_scr, dk_acc, dv_acc):
    qb = pl.program_id(0)
    n_q = pl.num_programs(0)
    seq = qkv_ref.shape[0]
    heads = qkv_ref.shape[1] // (3 * D)
    scale = D ** -0.5

    @pl.when(qb == 0)
    def _():
        seg = seg_ref[...]
        cut[0] = jnp.sum((seg < 1).astype(jnp.int32))
        cut[1] = jnp.sum((seg < 2).astype(jnp.int32))
        dk_acc[...] = jnp.zeros_like(dk_acc)
        dv_acc[...] = jnp.zeros_like(dv_acc)

    c1 = cut[0]
    c2 = cut[1]
    q0 = qb * BQ
    q1 = q0 + BQ - 1
    lo = jnp.where(q0 >= c2, c2, jnp.where(q0 >= c1, c1, 0))
    hi = jnp.where(q1 < c1, c1, jnp.where(q1 < c2, c2, seq))
    b_lo = lo // BK
    b_hi = (hi + BK - 1) // BK
    rows = pl.ds(pl.multiple_of(q0, BQ), BQ)
    iq = q0 + lax.broadcasted_iota(jnp.int32, (BQ, 1), 0)
    dq_doc = (iq >= c1).astype(jnp.int32) + (iq >= c2).astype(jnp.int32)
    q = [qkv_ref[rows, 3 * D * h:3 * D * h + D] for h in range(heads)]
    do = [do_ref[rows, D * h:D * h + D] for h in range(heads)]

    def first(kb, m):
        k0 = pl.multiple_of(kb * BK, BK)
        keys = pl.ds(k0, BK)
        ik = k0 + lax.broadcasted_iota(jnp.int32, (1, BK), 1)
        k_doc = (ik >= c1).astype(jnp.int32) + (ik >= c2).astype(jnp.int32)
        same = dq_doc == k_doc
        out = []
        for h in range(heads):
            k = qkv_ref[keys, 3 * D * h + D:3 * D * h + 2 * D]
            v = qkv_ref[keys, 3 * D * h + 2 * D:3 * D * h + 3 * D]
            s = lax.dot_general(q[h], k, NT, preferred_element_type=jnp.float32) * scale
            s = jnp.where(same, s, -jnp.inf)
            s_scr[h, :, keys] = s
            dp_scr[h, :, keys] = lax.dot_general(do[h], v, NT, preferred_element_type=jnp.float32)
            out.append(jnp.maximum(m[h], jnp.max(s, axis=1, keepdims=True)))
        return tuple(out)

    m = lax.fori_loop(b_lo, b_hi, first, tuple(jnp.full((BQ, 1), -jnp.inf, jnp.float32) for _ in range(heads)))

    def second(kb, ld):
        keys = pl.ds(pl.multiple_of(kb * BK, BK), BK)
        out = []
        for h in range(heads):
            p = jnp.exp(s_scr[h, :, keys] - m[h])
            s_scr[h, :, keys] = p
            l, dd = ld[h]
            out.append((l + jnp.sum(p, axis=1, keepdims=True), dd + jnp.sum(p * dp_scr[h, :, keys], axis=1, keepdims=True)))
        return tuple(out)

    zero = jnp.zeros((BQ, 1), jnp.float32)
    ld = lax.fori_loop(b_lo, b_hi, second, tuple((zero, zero) for _ in range(heads)))
    inv = [1.0 / ld[h][0] for h in range(heads)]
    row_dot = [ld[h][1] * inv[h] for h in range(heads)]
    inv_sc = [inv[h] * scale for h in range(heads)]

    def third(kb, acc):
        keys = pl.ds(pl.multiple_of(kb * BK, BK), BK)
        out = []
        for h in range(heads):
            k = qkv_ref[keys, 3 * D * h + D:3 * D * h + 2 * D]
            v = qkv_ref[keys, 3 * D * h + 2 * D:3 * D * h + 3 * D]
            p = s_scr[h, :, keys]
            p_bf = (p * inv[h]).astype(jnp.bfloat16)
            ds = ((p * inv_sc[h]) * (dp_scr[h, :, keys] - row_dot[h])).astype(jnp.bfloat16)
            o, dq = acc[h]
            o = o + jnp.dot(p_bf, v, preferred_element_type=jnp.float32)
            dq = dq + jnp.dot(ds, k, preferred_element_type=jnp.float32)
            dk_acc[h, keys, :] += lax.dot_general(ds, q[h], TN, preferred_element_type=jnp.float32)
            dv_acc[h, keys, :] += lax.dot_general(p_bf, do[h], TN, preferred_element_type=jnp.float32)
            out.append((o, dq))
        return tuple(out)

    zacc = jnp.zeros((BQ, D), jnp.float32)
    acc = lax.fori_loop(b_lo, b_hi, third, tuple((zacc, zacc) for _ in range(heads)))
    for h in range(heads):
        o_ref[rows, D * h:D * h + D] = acc[h][0].astype(jnp.bfloat16)
        dqkv_ref[rows, 3 * D * h:3 * D * h + D] = acc[h][1].astype(jnp.bfloat16)

    @pl.when(qb == n_q - 1)
    def _():
        for h in range(heads):
            dqkv_ref[:, 3 * D * h + D:3 * D * h + 2 * D] = dk_acc[h].astype(jnp.bfloat16)
            dqkv_ref[:, 3 * D * h + 2 * D:3 * D * h + 3 * D] = dv_acc[h].astype(jnp.bfloat16)

def attention(seg_row, qkv, d_attn):
    seq, width = qkv.shape
    heads = width // (3 * D)
    full = lambda shape: pl.BlockSpec(shape, lambda i: tuple(0 for _ in shape))
    return pl.pallas_call(
        attn_kernel,
        grid=(seq // BQ,),
        in_specs=[full(seg_row.shape), full(qkv.shape), full(d_attn.shape)],
        out_specs=[full(qkv.shape), full(d_attn.shape)],
        out_shape=[jax.ShapeDtypeStruct(qkv.shape, jnp.bfloat16), jax.ShapeDtypeStruct(d_attn.shape, jnp.bfloat16)],
        scratch_shapes=[
            pltpu.SMEM((2,), jnp.int32),
            pltpu.VMEM((heads, BQ, seq), jnp.float32),
            pltpu.VMEM((heads, BQ, seq), jnp.float32),
            pltpu.VMEM((heads, seq, D), jnp.float32),
            pltpu.VMEM((heads, seq, D), jnp.float32),
        ],
        compiler_params=pltpu.CompilerParams(dimension_semantics=("arbitrary",), vmem_limit_bytes=60 * 1024 * 1024),
    )(seg_row, qkv, d_attn)


def solution(mesh):
    tok_spec = P(('dp', 'row'), 'col')
    mat_spec = P('row', 'col')
    seg_spec = P(('dp', 'row'))

    def grad_step(x_blk, wqkv_blk, wout_blk, seg_blk, dy_blk):
        seq_loc, width_loc = x_blk.shape
        y = lax.axis_index('col')
        r = lax.axis_index('row')
        x_all = lax.all_gather(lax.all_gather(x_blk, 'col', axis=1, tiled=True), 'row', axis=0, tiled=True)
        dy_all = lax.all_gather(lax.all_gather(dy_blk, 'col', axis=1, tiled=True), 'row', axis=0, tiled=True)
        w_col = lax.all_gather(wqkv_blk, 'row', axis=0, tiled=True)
        wo_all = lax.all_gather(lax.all_gather(wout_blk, 'col', axis=1, tiled=True), 'row', axis=0, tiled=True)
        seg_all = lax.all_gather(seg_blk, 'row', axis=0, tiled=True)
        hw = w_col.shape[1] // 4
        ow = hw // 3
        w_h = lax.dynamic_slice_in_dim(w_col, r * hw, hw, 1)
        wo_h = lax.dynamic_slice_in_dim(wo_all, (y * 4 + r) * ow, ow, 0)
        qkv = jnp.dot(x_all, w_h, preferred_element_type=jnp.float32).astype(jnp.bfloat16)
        d_attn = lax.dot_general(dy_all, wo_h, NT, preferred_element_type=jnp.float32).astype(jnp.bfloat16)
        d_qkv, attn_out = attention(seg_all.reshape(-1, 128), qkv, d_attn)
        dw_h = lax.dot_general(x_all, d_qkv, TN, preferred_element_type=jnp.float32).astype(jnp.bfloat16)
        grad_wqkv = lax.all_to_all(dw_h, 'row', 0, 1, tiled=True)
        d_tok = lax.all_to_all(d_qkv, 'row', 0, 1, tiled=True)
        dx_part = lax.dot_general(d_tok, w_col, NT, preferred_element_type=jnp.float32)
        grad_x = lax.psum_scatter(dx_part, 'col', scatter_dimension=1, tiled=True).astype(jnp.bfloat16)
        dwo_h = lax.dot_general(attn_out, dy_all, TN, preferred_element_type=jnp.float32).astype(jnp.bfloat16)
        dwo_all = lax.all_gather(lax.all_gather(dwo_h, 'row', axis=0, tiled=True), 'col', axis=0, tiled=True)
        grad_wout = lax.dynamic_slice(dwo_all, (r * seq_loc, y * width_loc), (seq_loc, width_loc))
        return grad_x, grad_wqkv, grad_wout

    return jax.shard_map(grad_step, mesh=mesh, in_specs=(tok_spec, mat_spec, mat_spec, seg_spec, tok_spec), out_specs=(tok_spec, tok_spec, tok_spec), check_vma=False)
```

time: 865 us -> 661 us (0.76)
  matrix products: 211 us -> 45.7 us
  waiting for transfers between devices: 545 us -> 470 us
  other arithmetic: 65.6 us -> 2.72 us
  blocking collectives: 6.99 us -> 68.5 us
  Pallas kernels: 0 us -> 45.3 us
    reduce_scatter x4 -> x0, waiting for transfers between devices: 295 us -> none  [the longest x1 169 us: grad_step(): lax.psum_scatter(dw_part, 'row', scatter_dimension=0, tiled=True)]
    all_gather x4 -> x8, waiting for transfers between devices: 115 us -> 348 us  [the longest x1 96.3 us: grad_step(): lax.all_gather(lax.all_gather(dwo_h, 'row', axis=0, tiled=True), 'col', a...]
    dot_general x11 -> x5, matrix products: 211 us -> 45.7 us  [the longest x1 11.3 us: grad_step(): lax.dot_general(d_tok, w_col, NT, preferred_element_type=jnp.float32)]
    all_to_all x0 -> x1, blocking collectives: none -> 60.6 us  [grad_step(): d_tok = lax.all_to_all(d_qkv, 'row', 0, 1, tiled=True)]
    reduce_scatter x1, waiting for transfers between devices: 51.1 us -> 0.01 us  [grad_step(): lax.psum_scatter(dx_part, 'col', scatter_dimension=1, tiled=True)]
    pallas_call x0 -> x1, Pallas kernels: none -> 45.3 us  [attention(): pl.pallas_call(attn_kernel, grid=(seq // BQ,), in_specs=[full(seg_row.sha...]
    sub x1 -> x0, other arithmetic: 37.5 us -> none  [grad_step(): p_attn = jax.nn.softmax(scores, axis=-1)]
    all_to_all x0 -> x1, waiting for transfers between devices: none -> 36.7 us  [grad_step(): grad_wqkv = lax.all_to_all(dw_h, 'row', 0, 1, tiled=True)]
  transfers between devices with their start and end apart: 10 -> 11, of which waited for: 9 -> 9; matrix products, arithmetic and copies ran while one was open for 23% -> 6% of each run, Pallas kernels for 0% -> 0%
where the time goes in v1:
time: 661 us; the launch traced here: 662 us
  waiting for transfers between devices  470 us (71%)
  blocking collectives  68.5 us (10%)
  matrix products  45.7 us (7%)
  Pallas kernels  45.3 us (7%)
  between operations  14.2 us (2%)
  local copies, waits for them, and re-layouts  11.7 us (2%)
    all_gather x1, waiting for transfers between devices, grad_step(): lax.all_gather(lax.all_gather(dwo_h, 'row', axis=0, tiled=True), 'col', a...  96.3 us
    all_gather x1, waiting for transfers between devices, grad_step(): w_col = lax.all_gather(wqkv_blk, 'row', axis=0, tiled=True)  81.5 us
    all_to_all x1, blocking collectives, grad_step(): d_tok = lax.all_to_all(d_qkv, 'row', 0, 1, tiled=True)  60.6 us
    all_gather x1, waiting for transfers between devices, grad_step(): lax.all_gather(lax.all_gather(wout_blk, 'col', axis=1, tiled=True), 'row'...  57.1 us
    all_gather x1, waiting for transfers between devices, grad_step(): lax.all_gather(lax.all_gather(x_blk, 'col', axis=1, tiled=True), 'row', a...  50.1 us
    all_gather x1, waiting for transfers between devices, grad_step(): lax.all_gather(lax.all_gather(dy_blk, 'col', axis=1, tiled=True), 'row',...  48.4 us
    pallas_call x1, Pallas kernels, attention(): pl.pallas_call(attn_kernel, grid=(seq // BQ,), in_specs=[full(seg_row.sha...  45.3 us
    all_to_all x1, waiting for transfers between devices, grad_step(): grad_wqkv = lax.all_to_all(dw_h, 'row', 0, 1, tiled=True)  36.7 us
  transfers between devices with their start and end apart: 11, of which 9 were waited for; matrix products, arithmetic and copies ran while one was open for 6% of the time, Pallas kernels for 0%

profile of v1, /device:TPU:0, one launch (start us, length us, event | category | flops | bytes accessed | tf_op | source)
XLA Modules:
  0.0 661.8 jit_solution(14115676023096118459)
XLA Ops:
  7.2 0.0 all-gather.21.cloned.1.call-start
  7.2 0.7 all-gather.21.cloned.1.call-update
  7.9 0.0 all-gather.17.cloned.1.call-start
  7.9 0.7 all-gather.17.cloned.1.call-update
  8.6 0.0 all-gather.13.cloned.1.call-start
  8.7 0.7 all-gather.13.cloned.1.call-update
  9.4 0.0 all-gather.23.cloned.1.call-start
  9.4 33.1 %all-gather.21.cloned.1.call-done = bf16[512,2048]{1,0:T(8,128)(2,1)} async-done(((bf16[512,1024]{1,0:T(8,128)(2,1)}), bf16[512,2048]{1,0:T(8,128)(2,1)}) %all-gather.21.cloned.1.call-update) | async-done | bytes 2097168 | tf_op jit(solution)/shard_map/all_gather | solution.py:138
  42.5 0.0 all-gather.23.cloned.1.call-update
  42.5 0.0 copy-start.1
  42.5 0.0 all-gather.19.cloned.1.call-start
  42.6 31.6 %all-gather.17.cloned.1.call-done = bf16[512,2048]{1,0:T(8,128)(2,1)} async-done(((bf16[512,1024]{1,0:T(8,128)(2,1)}), bf16[512,2048]{1,0:T(8,128)(2,1)}) %all-gather.17.cloned.1.call-update) | async-done | bytes 2097168 | tf_op jit(solution)/shard_map/all_gather | solution.py:140
  74.2 0.0 all-gather.19.cloned.1.call-update
  74.2 0.0 all-gather.15.cloned.1.call-start
  74.2 31.6 %all-gather.13.cloned.1.call-done = bf16[512,2048]{1,0:T(8,128)(2,1)} async-done(((bf16[512,1024]{1,0:T(8,128)(2,1)}), bf16[512,2048]{1,0:T(8,128)(2,1)}) %all-gather.13.cloned.1.call-update) | async-done | bytes 2097168 | tf_op jit(solution)/shard_map/all_gather | solution.py:137
  105.9 0.0 all-gather.15.cloned.1.call-update
  105.9 0.0 all-gather.11.cloned.1.call-start
  105.9 0.7 all-gather.11.cloned.1.call-update
  106.6 0.0 all-gather.25.cloned.1.call-start
  106.7 0.0 copy-done.1
  106.7 7.9 %all-gather = s32[4,1,512]{2,1,0:T(1,128)} all-gather(s32[1,1,512]{2,1,0:T(1,128)S(1)} %bitcast.32), channel_id=1, replica_groups=mesh['dp'=1,'col'=2,'row'=4] {'row'}, dimensions={0}, use_global_device_ids=true | all-gather | bytes 10240 | tf_op jit(solution)/shard_map/all_gather | solution.py:141
  114.6 48.4 %all-gather.23.cloned.1.call-done = bf16[2048,2048]{1,0:T(8,128)(2,1)} async-done(((bf16[512,2048]{1,0:T(8,128)(2,1)}), bf16[2048,2048]{1,0:T(8,128)(2,1)}) %all-gather.23.cloned.1.call-update) | async-done | bytes 8388624 | tf_op jit(solution)/shard_map/all_gather | solution.py:138
  163.0 57.1 %all-gather.19.cloned.1.call-done = bf16[2048,2048]{1,0:T(8,128)(2,1)} async-done(((bf16[512,2048]{1,0:T(8,128)(2,1)}), bf16[2048,2048]{1,0:T(8,128)(2,1)}) %all-gather.19.cloned.1.call-update) | async-done | bytes 8388624 | tf_op jit(solution)/shard_map/all_gather | solution.py:140
  220.1 7.1 %fusion.4.do_ref = bf16[2048,256]{1,0:T(8,128)(2,1)} fusion(bf16[2048,2048]{1,0:T(8,128)(2,1)} %all-gather.23.cloned.1.call-done, bf16[2048,2048]{1,0:T(8,128)(2,1)} %all-gather.19.cloned.1.call-done, s32[]{:T(128)S(6)} %select_n.13), kind=kOutput, calls=%fused_computation.7 | convolution fusion | flops 2148007936 | bytes 10485764 | tf_op jit(solution)/shard_map/dot_general | solution.py:147
  227.2 50.1 %all-gather.15.cloned.1.call-done = bf16[2048,2048]{1,0:T(8,128)(2,1)} async-done(((bf16[512,2048]{1,0:T(8,128)(2,1)}), bf16[2048,2048]{1,0:T(8,128)(2,1)}) %all-gather.15.cloned.1.call-update) | async-done | bytes 8388624 | tf_op jit(solution)/shard_map/all_gather | solution.py:137
  277.3 81.5 %all-gather.11.cloned.1.call-done = bf16[2048,3072]{1,0:T(8,128)(2,1)} async-done(((bf16[512,3072]{1,0:T(8,128)(2,1)}), bf16[2048,3072]{1,0:T(8,128)(2,1)}) %all-gather.11.cloned.1.call-update) | async-done | bytes 12582928 | tf_op jit(solution)/shard_map/all_gather | solution.py:139
  358.8 11.1 %fusion.1.qkv_ref = bf16[2048,768]{1,0:T(8,128)(2,1)} fusion(bf16[2048,2048]{1,0:T(8,128)(2,1)} %all-gather.15.cloned.1.call-done, bf16[2048,3072]{1,0:T(8,128)(2,1)} %all-gather.11.cloned.1.call-done, s32[]{:T(128)S(6)} %select_n.12), kind=kOutput, calls=%fused_computation.4 | convolution fusion | flops 6444023808 | bytes 14680068 | tf_op jit(solution)/shard_map/dot_general | solution.py:146
  369.9 45.3 %shard_map.76 = (bf16[2048,768]{1,0:T(8,128)(2,1)}, bf16[2048,256]{1,0:T(8,128)(2,1)}) custom-call(s32[16,128]{1,0:T(8,128)} %bitcast.31, bf16[2048,768]{1,0:T(8,128)(2,1)} %fusion.1.qkv_ref, bf16[2048,256]{1,0:T(8,128)(2,1)} %fusion.4.do_ref), custom_call_target="tpu_custom_call" | custom-call | tf_op jit(solution)/shard_map/pallas_call | solution.py:111
  415.2 7.0 %convolution_convert_fusion.2 = bf16[256,2048]{1,0:T(8,128)(2,1)} fusion(bf16[2048,256]{1,0:T(8,128)(2,1)} %get-tuple-element.6, bf16[2048,2048]{1,0:T(8,128)(2,1)} %all-gather.23.cloned.1.call-done), kind=kOutput, calls=%fused_computation.5 | convolution fusion | flops 2148007936 | bytes 10485760 | tf_op jit(solution)/shard_map/dot_general | solution.py:154
  422.2 0.0 all-gather.25.cloned.1.call-update
  422.2 0.0 reduce-scatter.2.cloned.1.call-start
  422.3 3.2 copy.17
  425.5 60.6 %all_to_all.38 = bf16[4,512,768]{1,2,0:T(8,128)(2,1)S(1)} all-to-all(bf16[4,512,768]{1,2,0:T(8,128)(2,1)S(1)} %copy.17), channel_id=1, replica_groups=mesh['dp'=1,'col'=2,'row'=4] {'row'}, dimensions={0} | all-to-all | bytes 6291456 | tf_op jit(solution)/shard_map/all_to_all | solution.py:151
  486.1 11.3 %fusion.8 = f32[512,2048]{1,0:T(8,128)} fusion(bf16[512,3072]{0,1:T(8,128)(2,1)S(1)} %bitcast.29, bf16[2048,3072]{1,0:T(8,128)(2,1)} %all-gather.11.cloned.1.call-done), kind=kOutput, calls=%fused_computation.11 | convolution fusion | flops 6442450944 | bytes 19922944 | tf_op jit(solution)/shard_map/dot_general | solution.py:152
  497.4 0.0 copy-start
  497.4 0.0 reduce-scatter.2.cloned.1.call-update
  497.4 0.0 all-gather.27.cloned.1.call-start
  497.5 0.0 all-gather.25.cloned.1.call-done
  497.5 0.5 all-gather.27.cloned.1.call-update
  498.0 1.3 copy-done
  499.3 9.1 %convolution_convert_fusion.1 = bf16[768,2048]{1,0:T(8,128)(2,1)S(1)} fusion(bf16[2048,768]{1,0:T(8,128)(2,1)S(1)} %copy-done, bf16[2048,2048]{1,0:T(8,128)(2,1)} %all-gather.15.cloned.1.call-done), kind=kOutput, calls=%fused_computation.1 | convolution fusion | flops 6444023808 | bytes 14680064 | tf_op jit(solution)/shard_map/dot_general | solution.py:149
  508.4 1.9 copy.24
  510.3 3.7 all-to-all-start.1
  514.1 36.7 %all-to-all-done.1 = bf16[4,512,768]{1,2,0:T(8,128)(2,1)S(1)} async-done(((bf16[4,512,768]{1,2,0:T(8,128)(2,1)}), bf16[4,512,768]{1,2,0:T(8,128)(2,1)S(1)}, u32[]{:S(2)}, u32[]{:S(2)}) %all-to-all-start.1) | async-done | bytes 3145760 | tf_op jit(solution)/shard_map/all_to_all | solution.py:150
  550.7 3.0 copy.19
  553.7 2.7 convert_element_type.26
  556.5 96.3 %all-gather.27.cloned.1.call-done = bf16[2048,2048]{1,0:T(8,128)(2,1)} async-done(((bf16[1024,2048]{1,0:T(8,128)(2,1)}), bf16[2048,2048]{1,0:T(8,128)(2,1)}) %all-gather.27.cloned.1.call-update) | async-done | bytes 8388624 | tf_op jit(solution)/shard_map/all_gather | solution.py:155
  652.7 2.3 dynamic_slice.11
  (1 shorter events, 0.0 us)
Async XLA Ops:
  7.2 35.3 %all-gather.21.cloned.1.call-start = ((), (), s32[]{:S(2)}) async-start(), calls=%async_computation.8 | async-start | bytes 3145728 | tf_op jit(solution)/shard_map/all_gather | solution.py:138
  7.9 66.3 %all-gather.17.cloned.1.call-start = ((), (), s32[]{:S(2)}) async-start(), calls=%async_computation.6 | async-start | bytes 3145728 | tf_op jit(solution)/shard_map/all_gather | solution.py:140
  8.6 97.2 %all-gather.13.cloned.1.call-start = ((), (), s32[]{:S(2)}) async-start(), calls=%async_computation.4 | async-start | bytes 3145728 | tf_op jit(solution)/shard_map/all_gather | solution.py:137
  9.4 153.6 %all-gather.23.cloned.1.call-start = ((), (), s32[]{:S(2)}) async-start(), calls=%async_computation.9 | async-start | bytes 10485760 | tf_op jit(solution)/shard_map/all_gather | solution.py:138
  42.5 64.2 %copy-start.1 = (s32[512]{0:T(512)S(1)}, s32[512]{0:T(512)}, u32[]{:S(2)}) copy-start(s32[512]{0:T(512)} %param.8) | copy-start | bytes 6148
  42.5 177.6 %all-gather.19.cloned.1.call-start = ((), (), s32[]{:S(2)}) async-start(), calls=%async_computation.7 | async-start | bytes 10485760 | tf_op jit(solution)/shard_map/all_gather | solution.py:140
  74.2 203.1 %all-gather.15.cloned.1.call-start = ((), (), s32[]{:S(2)}) async-start(), calls=%async_computation.5 | async-start | bytes 10485760 | tf_op jit(solution)/shard_map/all_gather | solution.py:137
  105.9 252.9 %all-gather.11.cloned.1.call-start = ((), (), s32[]{:S(2)}) async-start(), calls=%async_computation.3 | async-start | bytes 15728640 | tf_op jit(solution)/shard_map/all_gather | solution.py:139
  106.6 390.9 %all-gather.25.cloned.1.call-start = ((), (), s32[]{:S(2)}) async-start(), calls=%async_computation.11 | async-start | bytes 5242880 | tf_op jit(solution)/shard_map/all_gather | solution.py:155
  422.2 131.5 %reduce-scatter.2.cloned.1.call-start = ((), (), s32[]{:S(2)}) async-start(), calls=%async_computation.10 | async-start | bytes 6291456 | tf_op jit(solution)/shard_map/reduce_scatter | solution.py:153
  497.4 1.9 copy-start
  497.4 155.3 %all-gather.27.cloned.1.call-start = ((), (), s32[]{:S(2)}) async-start(), calls=%async_computation.12 | async-start | bytes 12582912 | tf_op jit(solution)/shard_map/all_gather | solution.py:155
  510.3 40.4 %all-to-all-start.1 = ((bf16[4,512,768]{1,2,0:T(8,128)(2,1)}), bf16[4,512,768]{1,2,0:T(8,128)(2,1)S(1)}, u32[]{:S(2)}, u32[]{:S(2)}) async-start(bf16[4,512,768]{1,2,0:T(8,128)(2,1)} %bitcast.27), calls=%async_computation.2 | async-start | bytes 6291456 | tf_op jit(solution)/shard_map/all_to_all | solution.py:150
Sparse Core Ops, SparseCore 0:
  9.5 32.9 all-gather.20
  44.0 30.1 all-gather.16
  75.7 30.1 all-gather.12
  107.2 55.7 all-gather.22
  164.4 55.7 all-gather.18
  221.5 55.7 all-gather.14
  278.8 79.9 all-gather.10
  422.3 53.0 all-gather.24
  497.5 51.4 reduce-scatter.1
  550.4 102.2 all-gather.26

commit v2 on v0

v2 whole, which is shorter than its diff:
```python
import jax
import jax.numpy as jnp
from jax import lax
from jax.experimental import pallas as pl
from jax.experimental.pallas import tpu as pltpu
from jax.sharding import PartitionSpec as P

NT = (((1,), (1,)), ((), ()))
TN = (((0,), (0,)), ((), ()))
MESH = pl.DeviceIdType.MESH
BK = 512
D = 128
NC = 2
NJ = 2
LOW = -3.0e38
VMEM_LIMIT = 66_000_000


def mult(i, n):
    return pl.multiple_of(i * n, n)


def attention_block(q0, bq, h, c1, c2, qkv_v, do_v, p_scr, dp_scr, m_scr, kt, vt, dk_acc, dv_acc, dqkv_v, o_v):
    seq = qkv_v.shape[0]
    scale = D ** -0.5
    to_exp2 = scale * 1.4426950408889634
    f32 = jnp.float32
    rows = pl.ds(q0, bq)
    c0 = 3 * D * h
    iq = q0 + lax.broadcasted_iota(jnp.int32, (1, bq), 1)
    q_doc = (iq >= c1).astype(jnp.int32) + (iq >= c2).astype(jnp.int32)
    q = qkv_v[rows, c0:c0 + D]
    do = do_v[rows, D * h:D * h + D]

    def first(kb, carry):
        m, l, dd = carry
        k0 = pl.multiple_of(kb * BK, BK)
        keys = pl.ds(k0, BK)
        ik = k0 + lax.broadcasted_iota(jnp.int32, (BK, 1), 0)
        k_doc = (ik >= c1).astype(jnp.int32) + (ik >= c2).astype(jnp.int32)
        s = lax.dot_general(qkv_v[keys, c0 + D:c0 + 2 * D], q, NT, preferred_element_type=f32)
        s = jnp.where(q_doc == k_doc, s, LOW)
        dp = lax.dot_general(qkv_v[keys, c0 + 2 * D:c0 + 3 * D], do, NT, preferred_element_type=f32)
        dp_scr[keys, :] = dp
        m_new = jnp.maximum(m, jnp.max(s, axis=0, keepdims=True))
        p = jnp.exp2((s - m_new) * to_exp2)
        p_scr[keys, :] = p
        m_scr[kb] = m_new
        alpha = jnp.exp2((m - m_new) * to_exp2)
        return m_new, alpha * l + jnp.sum(p, axis=0, keepdims=True), alpha * dd + jnp.sum(p * dp, axis=0, keepdims=True)

    zero = jnp.zeros((1, bq), f32)
    m, l, dd = lax.fori_loop(0, seq // BK, first, (jnp.full((1, bq), LOW, f32), zero, zero))
    inv = 1.0 / l
    row_dot = dd * inv

    def second(kb, acc):
        o, dq = acc
        keys = pl.ds(pl.multiple_of(kb * BK, BK), BK)
        f = jnp.exp2((m_scr[kb] - m) * to_exp2) * inv
        p = p_scr[keys, :]
        p_bf = (p * f).astype(jnp.bfloat16)
        ds = ((p * (f * scale)) * (dp_scr[keys, :] - row_dot)).astype(jnp.bfloat16)
        o = o + jnp.dot(vt[h, :, keys], p_bf, preferred_element_type=f32)
        dq = dq + jnp.dot(kt[h, :, keys], ds, preferred_element_type=f32)
        dk_acc[h, keys, :] += jnp.dot(ds, q, preferred_element_type=f32)
        dv_acc[h, keys, :] += jnp.dot(p_bf, do, preferred_element_type=f32)
        return o, dq

    zacc = jnp.zeros((D, bq), f32)
    o, dq = lax.fori_loop(0, seq // BK, second, (zacc, zacc))
    o_v[rows, D * h:D * h + D] = o.T.astype(jnp.bfloat16)
    dqkv_v[rows, c0:c0 + D] = dq.T.astype(jnp.bfloat16)


def step_kernel(x_ref, w_ref, wo_ref, seg_ref, dy_ref, xg, dyg, dx_out, dw_out, dwo_out,
                w_v, tok, col_v, woh, qkv_v, do_v, seg_v, p_scr, dp_scr, m_scr, kt, vt, dk_acc, dv_acc, dqkv_v, o_v,
                dtok, dwo_v, px_recv, dx_v, relay, ssem, rsem, lsem):
    y = lax.axis_index('col')
    r = lax.axis_index('row')
    x = r // 2
    c = lax.rem(r, 2)
    r_s = r + 1 - 2 * c
    r_x = lax.rem(r + 2, 4)
    r_xs = lax.rem(r_s + 2, 4)
    sib, xn, yn = {'row': r_s}, {'row': r_x}, {'col': 1 - y}
    t_loc, h_loc = x_ref.shape
    hw = qkv_v.shape[1]
    ow = woh.shape[0]
    heads = ow // D
    ct, bt = t_loc // NC, t_loc // NJ
    f32, bf = jnp.float32, jnp.bfloat16
    started = []
    XB, YB, WB = 0, 7 * NC, 14 * NC
    WOB = WB + 12
    SGB = WOB + 2
    DQ = SGB + 3
    DW = DQ + 3 + 3 * NJ
    DWO = DW + 3
    PX = DWO + 2
    DWF = PX + NJ
    DWG = DWF + 1

    def copy(i, k, src, dst, dev):
        return pltpu.make_async_remote_copy(src, dst, ssem.at[i], rsem.at[k], device_id=dev, device_id_type=MESH)

    def send(i, src, dst, dev):
        cp = copy(i, i, src, dst, dev)
        cp.start()
        started.append(cp)

    def recv(i, dst):
        copy(i, i, dst, dst, sib).wait_recv()

    def local(i, src, dst):
        cp = pltpu.make_async_copy(src, dst, lsem.at[i])
        cp.start()
        return cp

    def slot(g, yy, rr, j):
        return g.at[pl.ds(pl.multiple_of(rr * t_loc + j * ct, ct), ct), pl.ds(mult(yy, h_loc), h_loc)]

    def tid(base, kind, j):
        return base + kind * NC + j

    def got_from(kind):
        return ((y, r_s), (y, r_x), (1 - y, r), (y, r_xs), (1 - y, r_x), (1 - y, r_s), (1 - y, r_xs))[kind]

    def send_own(a, g, base, kind, dev):
        for j in range(NC):
            send(tid(base, kind, j), a.at[pl.ds(j * ct, ct)], slot(g, y, r, j), dev)

    def forward(g, base, kind_in, outs, j):
        yy, rr = got_from(kind_in)
        recv(tid(base, kind_in, j), slot(g, yy, rr, j))
        for kind_out, dev in outs:
            send(tid(base, kind_out, j), slot(g, yy, rr, j), slot(g, yy, rr, j), dev)

    def take(g, base, kind):
        yy, rr = got_from(kind)
        for j in range(NC):
            recv(tid(base, kind, j), slot(g, yy, rr, j))

    def wslot(rr, q):
        return w_v.at[pl.ds(mult(rr, t_loc), t_loc), pl.ds(mult(q, hw), hw)]

    def wq(t, xx):
        return lax.rem(2 * xx + t, 4)

    def w_own(t, kind, xx, dev):
        q = wq(t, xx)
        send(WB + 4 * kind + t, w_ref.at[:, pl.ds(mult(q, hw), hw)], wslot(r, q), dev)

    def w_forward(t):
        q = wq(t, x)
        recv(WB + 4 + t, wslot(r_x, q))
        send(WB + 8 + t, wslot(r_x, q), wslot(r_x, q), sib)

    send_own(x_ref, xg, XB, 1, xn)
    send_own(x_ref, xg, XB, 2, yn)
    for t in range(2):
        w_own(t, 1, 1 - x, xn)
    send_own(x_ref, xg, XB, 0, sib)
    for t in range(4):
        w_own(t, 0, x, sib)
    for i, (rr, dev) in enumerate(((r_s, sib), (r_x, xn), (r_xs, {'row': r_xs}))):
        send(SGB + i, seg_ref, seg_v.at[r], dev)

    a = local(1, x_ref, tok.at[0, :, pl.ds(0, h_loc)])
    b = local(2, dy_ref, tok.at[1, :, pl.ds(0, h_loc)])
    d = local(3, w_ref, w_v.at[pl.ds(mult(r, t_loc), t_loc)])
    sg = local(4, seg_ref, seg_v.at[r])
    own_slot = lambda g: g.at[pl.ds(mult(r, t_loc), t_loc), pl.ds(mult(y, h_loc), h_loc)]
    a.wait()
    a = local(1, tok.at[0, :, pl.ds(0, h_loc)], own_slot(xg))
    b.wait()
    b = local(2, tok.at[1, :, pl.ds(0, h_loc)], own_slot(dyg))
    dk_acc[...] = jnp.zeros_like(dk_acc)
    dv_acc[...] = jnp.zeros_like(dv_acc)

    for j in range(NC):
        forward(xg, XB, 1, ((4, yn), (3, sib)), j)
        forward(xg, XB, 2, ((5, sib),), j)
    for k in range(2):
        row_to = 2 * c + k
        src = wo_ref.at[pl.ds(k * ow, ow)]
        dst = woh.at[:, pl.ds(mult(y, h_loc), h_loc)]
        mine = (x == y) & (row_to == r)

        @pl.when(mine)
        def _():
            pltpu.make_async_copy(src, dst, lsem.at[0]).start()

        @pl.when(jnp.logical_not(mine))
        def _():
            copy(WOB + k, WOB + y, src, dst, {'col': x, 'row': row_to}).start()
    send_own(dy_ref, dyg, YB, 2, yn)
    send_own(dy_ref, dyg, YB, 1, xn)
    send_own(dy_ref, dyg, YB, 0, sib)
    w_forward(0)
    for j in range(NC):
        forward(xg, XB, 4, ((6, sib),), j)
    a.wait()
    b.wait()
    d.wait()
    sg.wait()

    def load_tok(g, rr, s):
        return local(8 + s, g.at[pl.ds(mult(rr, t_loc), t_loc)], tok.at[s])

    blocks = (r, r_s, r_x, r_xs)
    for kind in (0, 3, 5, 6):
        take(xg, XB, kind)
    loads = [load_tok(xg, blocks[i], i) for i in range(2)]
    w_forward(1)
    for t in range(4):
        recv(WB + t, wslot(r_s, wq(t, x)))
    for t in range(2):
        recv(WB + 8 + t, wslot(r_xs, wq(t, x)))
    for i in range(4):
        loads[i].wait()
        rows = pl.ds(mult(blocks[i], t_loc), t_loc)
        for n in range(hw // 256):
            mine = w_v[:, pl.ds(pl.multiple_of(r * hw + 256 * n, 256), 256)]
            qkv_v[rows, 256 * n:256 * n + 256] = jnp.dot(tok[i % 2], mine, preferred_element_type=f32).astype(bf)
        if i < 2:
            loads.append(load_tok(xg, blocks[i + 2], i))
        for h in range(heads):
            kt[h, :, rows] = qkv_v[rows, 3 * D * h + D:3 * D * h + 2 * D].T
            vt[h, :, rows] = qkv_v[rows, 3 * D * h + 2 * D:3 * D * h + 3 * D].T

    for i, rr in enumerate((r_s, r_x, r_xs)):
        recv(SGB + i, seg_v.at[rr])
    c1 = jnp.sum((seg_v[...] < 1).astype(jnp.int32))
    c2 = jnp.sum((seg_v[...] < 2).astype(jnp.int32))
    for j in range(NC):
        forward(dyg, YB, 2, ((5, sib),), j)
    for yy in range(2):
        piece = woh.at[:, pl.ds(yy * h_loc, h_loc)]
        mine = (y == yy) & (2 * y + x == r)

        @pl.when(mine)
        def _():
            pltpu.make_async_copy(wo_ref.at[pl.ds(0, ow)], piece, lsem.at[0]).wait()

        @pl.when(jnp.logical_not(mine))
        def _():
            recv(WOB + yy, piece)

    def d_out(i, s):
        rows = pl.ds(mult(blocks[i], t_loc), t_loc)
        do_v[rows, :] = lax.dot_general(tok[s], woh[...], NT, preferred_element_type=f32).astype(bf)

    def attend(i, h):
        attention_block(mult(blocks[i], t_loc), t_loc, h, c1, c2, qkv_v, do_v, p_scr, dp_scr, m_scr, kt, vt, dk_acc, dv_acc, dqkv_v, o_v)

    def dy_forward(j):
        forward(dyg, YB, 1, ((4, yn), (3, sib)), j)

    load_tok(dyg, r, 0).wait()
    d_out(0, 0)
    attend(0, 0)
    dy_forward(0)
    attend(0, 1)
    dy_forward(1)
    for t in range(2, 4):
        w_own(t, 1, 1 - x, xn)
    for kind in (0, 5):
        take(dyg, YB, kind)
    load_tok(dyg, r_s, 1).wait()
    d_out(1, 1)
    attend(1, 0)
    forward(dyg, YB, 4, ((6, sib),), 0)
    attend(1, 1)
    forward(dyg, YB, 4, ((6, sib),), 1)
    load_tok(dyg, r_x, 0).wait()
    d_out(2, 0)
    attend(2, 0)
    w_forward(2)
    take(dyg, YB, 3)
    take(dyg, YB, 6)
    load_tok(dyg, r_xs, 1).wait()
    d_out(3, 1)
    ld = [local(5 + s, dyg.at[:, pl.ds(512 * s, 512)], col_v.at[s]) for s in range(2)]
    attend(3, 0)

    others = (r_s, r_x, r_xs)

    def finish(h):
        c0 = 3 * D * h
        dqkv_v[:, c0 + D:c0 + 2 * D] = dk_acc[h].astype(bf)
        dqkv_v[:, c0 + 2 * D:c0 + 3 * D] = dv_acc[h].astype(bf)

    def tok_slot(rr, h, j, n):
        return dtok.at[pl.ds(j * n, n), pl.ds(pl.multiple_of(rr * hw + 3 * D * h, 3 * D), 3 * D)]

    def send_dqkv(i, h, j, n):
        for k in (1, 2, 0):
            src = dqkv_v.at[pl.ds(pl.multiple_of(others[k] * t_loc + j * n, n), n), pl.ds(3 * D * h, 3 * D)]
            send(i + k, src, tok_slot(r, h, j, n), {'row': others[k]})

    finish(0)
    send_dqkv(DQ, 0, 0, t_loc)
    attend(2, 1)
    w_forward(3)
    attend(3, 1)
    finish(1)
    for j in range(NJ):
        send_dqkv(DQ + 3 + 3 * j, 1, j, bt)
    dtok[:, pl.ds(mult(r, hw), hw)] = dqkv_v[pl.ds(mult(r, t_loc), t_loc), :]

    order = (r_x, r_xs, r_s, r)
    for s in range(4):
        ld[s].wait()
        dwo_v[:, 512 * s:512 * s + 512] = lax.dot_general(o_v[...], col_v[s % 2], TN, preferred_element_type=f32).astype(bf)
        if s < 2:
            ld.append(local(5 + s, dyg.at[:, pl.ds(512 * s + 1024, 512)], col_v.at[s]))
        else:
            ld.append(local(5 + s - 2, xg.at[:, pl.ds(mult(order[s - 2], t_loc), t_loc)], col_v.at[s - 2]))
    ld = ld[4:]
    row_to = 2 * y + x
    near = x == y
    for k in range(2):
        src = dwo_v.at[:, pl.ds(k * h_loc, h_loc)]
        dst = dwo_out.at[pl.ds(mult(c, ow), ow)]
        mine = (y == k) & (row_to == r)
        far = (y != k) & (x != y)

        @pl.when(mine)
        def _():
            pltpu.make_async_copy(src, dst, lsem.at[0]).start()

        @pl.when(far)
        def _():
            copy(DWF, DWF, src, relay, {'col': k}).start()

        @pl.when(jnp.logical_not(mine | far))
        def _():
            copy(DWO + k, DWO + c, src, dst, {'col': k, 'row': row_to}).start()

    def dw_slot(rr):
        return dw_out.at[:, pl.ds(mult(rr, hw), hw)]

    def d_w(i):
        s = i % 2
        ld[i].wait()
        qkv_v[t_loc * i:t_loc * i + t_loc, :] = lax.dot_general(col_v[s], dqkv_v[...], TN, preferred_element_type=f32).astype(bf)
        if i < 2:
            ld.append(local(5 + s, xg.at[:, pl.ds(mult(order[i + 2], t_loc), t_loc)], col_v.at[s]))

    def send_dw(i, k):
        send(DW + k, qkv_v.at[pl.ds(t_loc * i, t_loc)], dw_slot(r), {'row': others[k]})

    def d_x(j, half, dst):
        for n in range(h_loc // 256):
            rows = pl.ds(pl.multiple_of(half * h_loc + 256 * n, 256), 256)
            dst[pl.ds(2 * bt * j + bt * (n // 2), bt), 256 * (n % 2):256 * (n % 2) + 256] = lax.dot_general(
                dtok[pl.ds(j * bt, bt), :], w_v[rows, :], NT, preferred_element_type=f32)

    def d_x_send(j):
        for k in range(3):
            recv(DQ + 3 + 3 * j + k, tok_slot(others[k], 1, j, bt))
        d_x(j, 1 - y, dp_scr)
        part = pl.ds(2 * bt * j, 2 * bt)
        send(PX + j, dp_scr.at[part], px_recv.at[part], yn)

    d_w(0)
    send_dw(0, 1)
    d_w(1)
    send_dw(1, 2)
    for t in range(2, 4):
        recv(WB + 8 + t, wslot(r_xs, wq(t, x)))
    for k in range(3):
        recv(DQ + k, tok_slot(others[k], 0, 0, t_loc))
    d_x_send(0)

    @pl.when(near)
    def _():
        recv(DWF, relay)
        copy(DWG, DWG + c, relay, dwo_out.at[pl.ds(mult(c, ow), ow)], {'row': 2 * (1 - y) + x}).start()

    d_w(2)
    send_dw(2, 0)
    d_x_send(1)
    d_x(0, y, p_scr)
    d_w(3)
    own_dw = local(7, qkv_v.at[pl.ds(3 * t_loc, t_loc)], dw_slot(r))
    d_x(1, y, p_scr)
    outs = []
    for j in range(NJ):
        recv(PX + j, px_recv.at[pl.ds(2 * bt * j, 2 * bt)])
        for q in range(2):
            part = pl.ds(2 * bt * j + bt * q, bt)
            dx_v[pl.ds(j * bt, bt), 512 * q:512 * q + 512] = (p_scr[part, :] + px_recv[part, :]).astype(bf)
        outs.append(local(8 + j, dx_v.at[pl.ds(j * bt, bt)], dx_out.at[pl.ds(j * bt, bt)]))
    own_dw.wait()
    for k in range(3):
        recv(DW + k, dw_slot(others[k]))
    src_col, src_x = r // 2, lax.rem(r, 2)
    for k in range(2):
        piece = dwo_out.at[pl.ds(k * ow, ow)]
        mine = (src_col == y) & (2 * src_x + k == r)
        far = (src_col != y) & (src_x != src_col)

        @pl.when(mine)
        def _():
            pltpu.make_async_copy(dwo_v.at[:, pl.ds(0, h_loc)], piece, lsem.at[0]).wait()

        @pl.when(far)
        def _():
            recv(DWG + k, piece)

        @pl.when(jnp.logical_not(mine | far))
        def _():
            recv(DWO + k, piece)
    for cp in outs:
        cp.wait()
    for cp in started:
        cp.wait_send()
    half = dwo_v.at[:, pl.ds(0, h_loc)]
    for k in range(2):
        @pl.when(jnp.logical_not((x == y) & (2 * c + k == r)))
        def _():
            copy(WOB + k, WOB + k, wo_ref.at[pl.ds(0, ow)], half, sib).wait_send()

        @pl.when(jnp.logical_not(((y == k) & (row_to == r)) | ((y != k) & (x != y))))
        def _():
            copy(DWO + k, DWO + k, half, relay, sib).wait_send()

    @pl.when(jnp.logical_not(near))
    def _():
        copy(DWF, DWF, half, relay, yn).wait_send()

    @pl.when(near)
    def _():
        copy(DWG, DWG, relay, relay, sib).wait_send()


def step_all(x_blk, w_blk, wo_blk, seg_blk, dy_blk):
    t_loc, h_loc = x_blk.shape
    w_loc = w_blk.shape[1]
    seq, hid = 4 * t_loc, 2 * h_loc
    hw, ow = w_loc // 4, w_loc // 12
    heads = ow // D
    bf, f32 = jnp.bfloat16, jnp.float32
    hbm = pl.BlockSpec(memory_space=pl.ANY)
    n_sem = 14 * NC + 12 + 2 + 3 + 3 + 3 * NJ + 3 + 2 + NJ + 1 + 2
    return pl.pallas_call(
        step_kernel,
        in_specs=[hbm] * 5,
        out_specs=[hbm] * 5,
        out_shape=[jax.ShapeDtypeStruct((seq, hid), bf)] * 2 + [jax.ShapeDtypeStruct(b.shape, bf) for b in (x_blk, w_blk, wo_blk)],
        scratch_shapes=[
            pltpu.VMEM((hid, w_loc), bf), pltpu.VMEM((2, t_loc, hid), bf), pltpu.VMEM((2, seq, t_loc), bf),
            pltpu.VMEM((ow, hid), bf), pltpu.VMEM((seq, hw), bf), pltpu.VMEM((seq, ow), bf),
            pltpu.VMEM((4,) + seg_blk.shape, jnp.int32),
            pltpu.VMEM((seq, t_loc), f32), pltpu.VMEM((seq, t_loc), f32), pltpu.VMEM((seq // BK, 1, t_loc), f32),
            pltpu.VMEM((heads, D, seq), bf), pltpu.VMEM((heads, D, seq), bf),
            pltpu.VMEM((heads, seq, D), f32), pltpu.VMEM((heads, seq, D), f32),
            pltpu.VMEM((seq, hw), bf), pltpu.VMEM((seq, ow), bf),
            pltpu.VMEM((t_loc, w_loc), bf), pltpu.VMEM((ow, hid), bf), pltpu.VMEM((2 * t_loc, t_loc), f32),
            pltpu.VMEM((t_loc, h_loc), bf), pltpu.VMEM((ow, h_loc), bf),
            pltpu.SemaphoreType.DMA((n_sem,)), pltpu.SemaphoreType.DMA((n_sem,)), pltpu.SemaphoreType.DMA((10,)),
        ],
        compiler_params=pltpu.CompilerParams(has_side_effects=True, vmem_limit_bytes=VMEM_LIMIT),
        name='mega_step',
    )(x_blk, w_blk, wo_blk, seg_blk, dy_blk)


def solution(mesh):
    tok_spec = P(('dp', 'row'), 'col')
    mat_spec = P('row', 'col')
    seg_spec = P(('dp', 'row'))

    def grad_step(x_blk, wqkv_blk, wout_blk, seg_blk, dy_blk):
        _, _, grad_x, grad_wqkv, grad_wout = step_all(x_blk, wqkv_blk, wout_blk, seg_blk.reshape(4, -1), dy_blk)
        return grad_x, grad_wqkv, grad_wout

    return jax.shard_map(grad_step, mesh=mesh, in_specs=(tok_spec, mat_spec, mat_spec, seg_spec, tok_spec), out_specs=(tok_spec, tok_spec, tok_spec), check_vma=False)
```

time: 865 us -> 222 us (0.26)
  waiting for transfers between devices: 545 us -> 0 us
  Pallas kernels: 0 us -> 214 us
  matrix products: 211 us -> 0 us
  other arithmetic: 65.6 us -> 0 us
  between operations: 14.7 us -> 0.64 us
  local copies, waits for them, and re-layouts: 16 us -> 7.08 us
    reduce_scatter x5 -> x0, waiting for transfers between devices: 347 us -> none  [the longest x1 169 us: grad_step(): lax.psum_scatter(dw_part, 'row', scatter_dimension=0, tiled=True)]
    pallas_call x0 -> x1, Pallas kernels: none -> 214 us  [step_all(): pl.pallas_call(step_kernel, in_specs=[hbm] * 5, out_specs=[hbm] * 5, out_...]
    dot_general x11 -> x0, matrix products: 211 us -> none  [the longest x1 48.7 us: grad_step(): jnp.einsum('hqk,qhd->khd', d_scores, q_loc, preferred_element_type=jnp.fl...]
    all_gather x5 -> x0, waiting for transfers between devices: 196 us -> none  [the longest x1 81.5 us: grad_step(): w_col = lax.all_gather(wqkv_blk, 'row', axis=0, tiled=True)]
    sub x1 -> x0, other arithmetic: 37.5 us -> none  [grad_step(): p_attn = jax.nn.softmax(scores, axis=-1)]
    another operation x2 -> x0, other arithmetic: 14.2 us -> none  [the longest x1 11.7 us: grad_step(): jnp.stack([dk_part, dv_part], axis=2)]
    convert_element_type x4 -> x0, other arithmetic: 12 us -> none  [the longest x1 4.82 us: grad_step(): lax.psum_scatter(dw_part, 'row', scatter_dimension=0, tiled=True)]
  transfers between devices with their start and end apart: 10 -> 0, of which waited for: 9 -> 0; matrix products, arithmetic and copies ran while one was open for 23% -> 0% of each run, Pallas kernels for 0% -> 0%
where the time goes in v2:
time: 222 us
  Pallas kernels  214 us (96%)
  local copies, waits for them, and re-layouts  7.08 us (3%)
    pallas_call x1, Pallas kernels, step_all(): pl.pallas_call(step_kernel, in_specs=[hbm] * 5, out_specs=[hbm] * 5, out_...  214 us
    unnamed x5, local copies, waits for them, and re-layouts  7.08 us

profile of v2, /device:TPU:0, one launch (start us, length us, event | category | flops | bytes accessed | tf_op | source)
XLA Modules:
  0.0 222.0 jit_solution(7998312522405210785)
XLA Ops:
  0.6 214.3 %mega_step.1 = (bf16[2048,2048]{1,0:T(8,128)(2,1)}, bf16[2048,2048]{1,0:T(8,128)(2,1)}, bf16[512,1024]{1,0:T(8,128)(2,1)}, bf16[512,3072]{1,0:T(8,128)(2,1)}, bf16[512,1024]{1,0:T(8,128)(2,1)}) custom-call(bf16[512,1024]{1,0:T(8,128)(2,1)} %x_ref.1, bf16[512,3072]{1,0:T(8,128)(2,1)} %w_ref.1, bf16[512,1024]{1,0:T(8,128)(2,1)} %wo_ref.1, s32[4,128]{1,0:T(4,128)} %bitcast.1, ...), custom_call_target="tpu_custom_call" | custom-call | tf_op jit(solution)/shard_map/mega_step/pallas_call | solution.py:448
  214.9 2.3 %copy.11 = bf16[512,1024]{1,0:T(8,128)(2,1)} copy(bf16[512,1024]{1,0:T(8,128)(2,1)} %get-tuple-element.12) | data formatting | bytes 2097152
  217.2 0.0 copy-start
  217.2 3.8 %copy.12 = bf16[512,3072]{1,0:T(8,128)(2,1)} copy(bf16[512,3072]{1,0:T(8,128)(2,1)} %get-tuple-element.13) | data formatting | bytes 6291456
  221.0 0.0 copy-done
  221.0 1.0 copy.13
Async XLA Ops:
  217.2 3.8 %copy-start = (bf16[512,1024]{1,0:T(8,128)(2,1)S(1)}, bf16[512,1024]{1,0:T(8,128)(2,1)}, u32[]{:S(2)}) copy-start(bf16[512,1024]{1,0:T(8,128)(2,1)} %get-tuple-element.14) | copy-start | bytes 3145732

commit v3 on v2

--- a/solution.py
+++ b/solution.py
@@ -1,3 +1,5 @@
+import functools
+
 import jax
 import jax.numpy as jnp
 from jax import lax
@@ -20,7 +22,7 @@
     return pl.multiple_of(i * n, n)
 
 
-def attention_block(q0, bq, h, c1, c2, qkv_v, do_v, p_scr, dp_scr, m_scr, kt, vt, dk_acc, dv_acc, dqkv_v, o_v):
+def attention_block(q0, bq, h, c1, c2, qkv_v, do_v, p_scr, dp_scr, m_scr, kt, vt, dk_acc, dv_acc, dqkv_v, o_v, between):
     seq = qkv_v.shape[0]
     scale = D ** -0.5
     to_exp2 = scale * 1.4426950408889634
@@ -51,6 +53,8 @@
 
     zero = jnp.zeros((1, bq), f32)
     m, l, dd = lax.fori_loop(0, seq // BK, first, (jnp.full((1, bq), LOW, f32), zero, zero))
+    if between is not None:
+        between()
     inv = 1.0 / l
     row_dot = dd * inv
 
@@ -156,6 +160,11 @@
         recv(WB + 4 + t, wslot(r_x, q))
         send(WB + 8 + t, wslot(r_x, q), wslot(r_x, q), sib)
 
+    barrier = pltpu.get_barrier_semaphore()
+    for i in range(1, 8):
+        pl.semaphore_signal(barrier, inc=1, device_id={'row': lax.rem(r + i, 4), 'col': lax.rem(y + i // 4, 2)}, device_id_type=MESH)
+    pl.semaphore_wait(barrier, 7)
+
     send_own(x_ref, xg, XB, 1, xn)
     send_own(x_ref, xg, XB, 2, yn)
     for t in range(2):
@@ -251,20 +260,18 @@
         rows = pl.ds(mult(blocks[i], t_loc), t_loc)
         do_v[rows, :] = lax.dot_general(tok[s], woh[...], NT, preferred_element_type=f32).astype(bf)
 
-    def attend(i, h):
-        attention_block(mult(blocks[i], t_loc), t_loc, h, c1, c2, qkv_v, do_v, p_scr, dp_scr, m_scr, kt, vt, dk_acc, dv_acc, dqkv_v, o_v)
+    def attend(i, h, between=None):
+        attention_block(mult(blocks[i], t_loc), t_loc, h, c1, c2, qkv_v, do_v, p_scr, dp_scr, m_scr, kt, vt, dk_acc, dv_acc, dqkv_v, o_v, between)
 
     def dy_forward(j):
         forward(dyg, YB, 1, ((4, yn), (3, sib)), j)
 
     load_tok(dyg, r, 0).wait()
     d_out(0, 0)
-    attend(0, 0)
-    dy_forward(0)
-    attend(0, 1)
-    dy_forward(1)
+    attend(0, 0, lambda: dy_forward(0))
     for t in range(2, 4):
         w_own(t, 1, 1 - x, xn)
+    attend(0, 1, lambda: dy_forward(1))
     for kind in (0, 5):
         take(dyg, YB, kind)
     load_tok(dyg, r_s, 1).wait()
@@ -460,11 +467,44 @@
             pltpu.VMEM((seq, hw), bf), pltpu.VMEM((seq, ow), bf),
             pltpu.VMEM((t_loc, w_loc), bf), pltpu.VMEM((ow, hid), bf), pltpu.VMEM((2 * t_loc, t_loc), f32),
             pltpu.VMEM((t_loc, h_loc), bf), pltpu.VMEM((ow, h_loc), bf),
-            pltpu.SemaphoreType.DMA((n_sem,)), pltpu.SemaphoreType.DMA((n_sem,)), pltpu.SemaphoreType.DMA((10,)),
+            pltpu.SemaphoreType.DMA((n_sem,)), pltpu.SemaphoreType.DMA((n_sem,)), pltpu.SemaphoreType.DMA((16,)),
         ],
-        compiler_params=pltpu.CompilerParams(has_side_effects=True, vmem_limit_bytes=VMEM_LIMIT),
+        compiler_params=pltpu.CompilerParams(collective_id=0, has_side_effects=True, vmem_limit_bytes=VMEM_LIMIT),
         name='mega_step',
     )(x_blk, w_blk, wo_blk, seg_blk, dy_blk)
+
+
+def copy_kernel(parts, *refs):
+    n = len(parts)
+    ins, outs, bufs, sem_in, sem_out = refs[:n], refs[n:2 * n], refs[2 * n:3 * n], refs[3 * n], refs[3 * n + 1]
+    moves = []
+    for i in range(n):
+        step = ins[i].shape[0] // parts[i]
+        for j in range(parts[i]):
+            rows = pl.ds(j * step, step)
+            load = pltpu.make_async_copy(ins[i].at[rows], bufs[i].at[rows], sem_in.at[len(moves)])
+            load.start()
+            moves.append((load, pltpu.make_async_copy(bufs[i].at[rows], outs[i].at[rows], sem_out.at[len(moves)])))
+    for load, store in moves:
+        load.wait()
+        store.start()
+    for _, store in moves:
+        store.wait()
+
+
+def copy_out(*arrays):
+    parts = [a.shape[0] // 128 for a in arrays]
+    hbm = pl.BlockSpec(memory_space=pl.ANY)
+    shapes = [jax.ShapeDtypeStruct(a.shape, a.dtype) for a in arrays]
+    return pl.pallas_call(
+        functools.partial(copy_kernel, parts),
+        in_specs=[hbm] * len(arrays),
+        out_specs=[hbm] * len(arrays),
+        out_shape=shapes,
+        scratch_shapes=[pltpu.VMEM(a.shape, a.dtype) for a in arrays] + [pltpu.SemaphoreType.DMA((sum(parts),))] * 2,
+        compiler_params=pltpu.CompilerParams(vmem_limit_bytes=VMEM_LIMIT),
+        name='copy_out',
+    )(*arrays)
 
 
 def solution(mesh):
@@ -474,6 +514,6 @@
 
     def grad_step(x_blk, wqkv_blk, wout_blk, seg_blk, dy_blk):
         _, _, grad_x, grad_wqkv, grad_wout = step_all(x_blk, wqkv_blk, wout_blk, seg_blk.reshape(4, -1), dy_blk)
-        return grad_x, grad_wqkv, grad_wout
+        return copy_out(grad_x, grad_wqkv, grad_wout)
 
     return jax.shard_map(grad_step, mesh=mesh, in_specs=(tok_spec, mat_spec, mat_spec, seg_spec, tok_spec), out_specs=(tok_spec, tok_spec, tok_spec), check_vma=False)

time: 222 us -> 215 us (0.968)
  local copies, waits for them, and re-layouts: 7.08 us -> 0 us
    unnamed x5 -> x0, local copies, waits for them, and re-layouts: 7.08 us -> none
    pallas_call x1, Pallas kernels: 214 us -> 210 us  [step_all(): pl.pallas_call(step_kernel, in_specs=[hbm] * 5, out_specs=[hbm] * 5, out_...]
    pallas_call x0 -> x1, Pallas kernels: none -> 4.59 us  [copy_out(): pl.pallas_call(functools.partial(copy_kernel, parts), in_specs=[hbm] * le...]
where the time goes in v3:
time: 215 us
  Pallas kernels  214 us (100%)
    pallas_call x1, Pallas kernels, step_all(): pl.pallas_call(step_kernel, in_specs=[hbm] * 5, out_specs=[hbm] * 5, out_...  210 us
    pallas_call x1, Pallas kernels, copy_out(): pl.pallas_call(functools.partial(copy_kernel, parts), in_specs=[hbm] * le...  4.59 us

profile of v3, /device:TPU:0, one launch (start us, length us, event | category | flops | bytes accessed | tf_op | source)
XLA Modules:
  0.0 215.0 jit_solution(14285776815636651297)
XLA Ops:
  0.6 209.6 %mega_step.1 = (bf16[2048,2048]{1,0:T(8,128)(2,1)}, bf16[2048,2048]{1,0:T(8,128)(2,1)}, bf16[512,1024]{1,0:T(8,128)(2,1)}, bf16[512,3072]{1,0:T(8,128)(2,1)}, bf16[512,1024]{1,0:T(8,128)(2,1)}) custom-call(bf16[512,1024]{1,0:T(8,128)(2,1)} %x_ref.1, bf16[512,3072]{1,0:T(8,128)(2,1)} %w_ref.1, bf16[512,1024]{1,0:T(8,128)(2,1)} %wo_ref.1, s32[4,128]{1,0:T(4,128)} %bitcast.1, ...), custom_call_target="tpu_custom_call" | custom-call | tf_op jit(solution)/shard_map/mega_step/pallas_call | solution.py:455
  210.3 4.6 %copy_out.1 = (bf16[512,1024]{1,0:T(8,128)(2,1)}, bf16[512,3072]{1,0:T(8,128)(2,1)}, bf16[512,1024]{1,0:T(8,128)(2,1)}) custom-call(bf16[512,1024]{1,0:T(8,128)(2,1)} %get-tuple-element.6.refs_0_, bf16[512,3072]{1,0:T(8,128)(2,1)} %get-tuple-element.7.refs_1_, bf16[512,1024]{1,0:T(8,128)(2,1)} %get-tuple-element.8.refs_2_), custom_call_target="tpu_custom_call" | custom-call | tf_op jit(solution)/shard_map/copy_out/pallas_call | solution.py:499

commit v4 on v3

--- a/solution.py
+++ b/solution.py
@@ -16,6 +16,7 @@
 NJ = 2
 LOW = -3.0e38
 VMEM_LIMIT = 66_000_000
+STEP_LIMIT = 57_000_000
 
 
 def mult(i, n):
@@ -79,7 +80,7 @@
 
 def step_kernel(x_ref, w_ref, wo_ref, seg_ref, dy_ref, xg, dyg, dx_out, dw_out, dwo_out,
                 w_v, tok, col_v, woh, qkv_v, do_v, seg_v, p_scr, dp_scr, m_scr, kt, vt, dk_acc, dv_acc, dqkv_v, o_v,
-                dtok, dwo_v, px_recv, dx_v, relay, ssem, rsem, lsem):
+                dtok, dwo_v, px_recv, relay, ssem, rsem, lsem):
     y = lax.axis_index('col')
     r = lax.axis_index('row')
     x = r // 2
@@ -104,6 +105,7 @@
     PX = DWO + 2
     DWF = PX + NJ
     DWG = DWF + 1
+    DQE = DWG + 2
 
     def copy(i, k, src, dst, dev):
         return pltpu.make_async_remote_copy(src, dst, ssem.at[i], rsem.at[k], device_id=dev, device_id_type=MESH)
@@ -216,6 +218,10 @@
 
     def load_tok(g, rr, s):
         return local(8 + s, g.at[pl.ds(mult(rr, t_loc), t_loc)], tok.at[s])
+
+    def load_half(g, yy, rr, s, i):
+        cols = pl.ds(mult(yy, h_loc), h_loc)
+        return local(i, g.at[pl.ds(mult(rr, t_loc), t_loc), cols], tok.at[s, :, cols])
 
     blocks = (r, r_s, r_x, r_xs)
     for kind in (0, 3, 5, 6):
@@ -238,12 +244,14 @@
             kt[h, :, rows] = qkv_v[rows, 3 * D * h + D:3 * D * h + 2 * D].T
             vt[h, :, rows] = qkv_v[rows, 3 * D * h + 2 * D:3 * D * h + 3 * D].T
 
+    near_half = load_half(dyg, y, r, 0, 10)
     for i, rr in enumerate((r_s, r_x, r_xs)):
         recv(SGB + i, seg_v.at[rr])
     c1 = jnp.sum((seg_v[...] < 1).astype(jnp.int32))
     c2 = jnp.sum((seg_v[...] < 2).astype(jnp.int32))
     for j in range(NC):
         forward(dyg, YB, 2, ((5, sib),), j)
+    far_half = load_half(dyg, 1 - y, r, 0, 11)
     for yy in range(2):
         piece = woh.at[:, pl.ds(yy * h_loc, h_loc)]
         mine = (y == yy) & (2 * y + x == r)
@@ -266,31 +274,12 @@
     def dy_forward(j):
         forward(dyg, YB, 1, ((4, yn), (3, sib)), j)
 
-    load_tok(dyg, r, 0).wait()
+    near_half.wait()
+    far_half.wait()
     d_out(0, 0)
     attend(0, 0, lambda: dy_forward(0))
     for t in range(2, 4):
         w_own(t, 1, 1 - x, xn)
-    attend(0, 1, lambda: dy_forward(1))
-    for kind in (0, 5):
-        take(dyg, YB, kind)
-    load_tok(dyg, r_s, 1).wait()
-    d_out(1, 1)
-    attend(1, 0)
-    forward(dyg, YB, 4, ((6, sib),), 0)
-    attend(1, 1)
-    forward(dyg, YB, 4, ((6, sib),), 1)
-    load_tok(dyg, r_x, 0).wait()
-    d_out(2, 0)
-    attend(2, 0)
-    w_forward(2)
-    take(dyg, YB, 3)
-    take(dyg, YB, 6)
-    load_tok(dyg, r_xs, 1).wait()
-    d_out(3, 1)
-    ld = [local(5 + s, dyg.at[:, pl.ds(512 * s, 512)], col_v.at[s]) for s in range(2)]
-    attend(3, 0)
-
     others = (r_s, r_x, r_xs)
 
     def finish(h):
@@ -298,13 +287,51 @@
         dqkv_v[:, c0 + D:c0 + 2 * D] = dk_acc[h].astype(bf)
         dqkv_v[:, c0 + 2 * D:c0 + 3 * D] = dv_acc[h].astype(bf)
 
-    def tok_slot(rr, h, j, n):
-        return dtok.at[pl.ds(j * n, n), pl.ds(pl.multiple_of(rr * hw + 3 * D * h, 3 * D), 3 * D)]
+    def tok_slot(rr, h, j, n, c0=0, c1=3 * D):
+        return dtok.at[pl.ds(j * n, n), pl.ds(pl.multiple_of(rr * hw + 3 * D * h + c0, D), c1 - c0)]
 
     def send_dqkv(i, h, j, n):
         for k in (1, 2, 0):
-            src = dqkv_v.at[pl.ds(pl.multiple_of(others[k] * t_loc + j * n, n), n), pl.ds(3 * D * h, 3 * D)]
-            send(i + k, src, tok_slot(r, h, j, n), {'row': others[k]})
+            c0 = D if (h, k) == (0, 1) else 0
+            src = dqkv_v.at[pl.ds(pl.multiple_of(others[k] * t_loc + j * n, n), n), pl.ds(3 * D * h + c0, 3 * D - c0)]
+            send(i + k, src, tok_slot(r, h, j, n, c0), {'row': others[k]})
+
+    def send_early_dq():
+        src = dqkv_v.at[pl.ds(mult(r_x, t_loc), t_loc), pl.ds(0, D)]
+        send(DQE, src, tok_slot(r, 0, 0, t_loc, 0, D), xn)
+
+    loading = []
+
+    def second_block():
+        dy_forward(1)
+        for kind in (0, 5):
+            take(dyg, YB, kind)
+        loading.append(load_tok(dyg, r_s, 1))
+
+    def last_block():
+        take(dyg, YB, 3)
+        take(dyg, YB, 6)
+        loading.append(load_tok(dyg, r_xs, 1))
+
+    attend(0, 1, second_block)
+    loading.pop().wait()
+    d_out(1, 1)
+    attend(1, 0)
+    forward(dyg, YB, 4, ((6, sib),), 0)
+    near_half = load_half(dyg, y, r_x, 0, 10)
+    attend(1, 1)
+    forward(dyg, YB, 4, ((6, sib),), 1)
+    far_half = load_half(dyg, 1 - y, r_x, 0, 11)
+    near_half.wait()
+    far_half.wait()
+    d_out(2, 0)
+    attend(2, 0, last_block)
+    send_early_dq()
+    w_forward(2)
+    loading.pop().wait()
+    d_out(3, 1)
+    ld = [local(5 + s, dyg.at[:, pl.ds(512 * s, 512)], col_v.at[s]) for s in range(2)]
+    attend(3, 0)
 
     finish(0)
     send_dqkv(DQ, 0, 0, t_loc)
@@ -351,7 +378,11 @@
     def d_w(i):
         s = i % 2
         ld[i].wait()
-        qkv_v[t_loc * i:t_loc * i + t_loc, :] = lax.dot_general(col_v[s], dqkv_v[...], TN, preferred_element_type=f32).astype(bf)
+        part = lax.dot_general(col_v[s], dqkv_v[...], TN, preferred_element_type=f32).astype(bf)
+        if i < 3:
+            qkv_v[t_loc * i:t_loc * i + t_loc, :] = part
+        else:
+            dw_out[:, pl.ds(mult(r, hw), hw)] = part
         if i < 2:
             ld.append(local(5 + s, xg.at[:, pl.ds(mult(order[i + 2], t_loc), t_loc)], col_v.at[s]))
 
@@ -377,8 +408,9 @@
     send_dw(1, 2)
     for t in range(2, 4):
         recv(WB + 8 + t, wslot(r_xs, wq(t, x)))
+    recv(DQE, tok_slot(r_x, 0, 0, t_loc, 0, D))
     for k in range(3):
-        recv(DQ + k, tok_slot(others[k], 0, 0, t_loc))
+        recv(DQ + k, tok_slot(others[k], 0, 0, t_loc, D if k == 1 else 0))
     d_x_send(0)
 
     @pl.when(near)
@@ -391,16 +423,12 @@
     d_x_send(1)
     d_x(0, y, p_scr)
     d_w(3)
-    own_dw = local(7, qkv_v.at[pl.ds(3 * t_loc, t_loc)], dw_slot(r))
     d_x(1, y, p_scr)
-    outs = []
     for j in range(NJ):
         recv(PX + j, px_recv.at[pl.ds(2 * bt * j, 2 * bt)])
         for q in range(2):
             part = pl.ds(2 * bt * j + bt * q, bt)
-            dx_v[pl.ds(j * bt, bt), 512 * q:512 * q + 512] = (p_scr[part, :] + px_recv[part, :]).astype(bf)
-        outs.append(local(8 + j, dx_v.at[pl.ds(j * bt, bt)], dx_out.at[pl.ds(j * bt, bt)]))
-    own_dw.wait()
+            dx_out[pl.ds(j * bt, bt), 512 * q:512 * q + 512] = (p_scr[part, :] + px_recv[part, :]).astype(bf)
     for k in range(3):
         recv(DW + k, dw_slot(others[k]))
     src_col, src_x = r // 2, lax.rem(r, 2)
@@ -420,8 +448,6 @@
         @pl.when(jnp.logical_not(mine | far))
         def _():
             recv(DWO + k, piece)
-    for cp in outs:
-        cp.wait()
     for cp in started:
         cp.wait_send()
     half = dwo_v.at[:, pl.ds(0, h_loc)]
@@ -451,12 +477,12 @@
     heads = ow // D
     bf, f32 = jnp.bfloat16, jnp.float32
     hbm = pl.BlockSpec(memory_space=pl.ANY)
-    n_sem = 14 * NC + 12 + 2 + 3 + 3 + 3 * NJ + 3 + 2 + NJ + 1 + 2
+    n_sem = 14 * NC + 12 + 2 + 3 + 3 + 3 * NJ + 3 + 2 + NJ + 1 + 2 + 1
     return pl.pallas_call(
         step_kernel,
         in_specs=[hbm] * 5,
-        out_specs=[hbm] * 5,
-        out_shape=[jax.ShapeDtypeStruct((seq, hid), bf)] * 2 + [jax.ShapeDtypeStruct(b.shape, bf) for b in (x_blk, w_blk, wo_blk)],
+        out_specs=[hbm] * 2 + [pl.BlockSpec(memory_space=pltpu.VMEM)] * 3,
+        out_shape=[jax.ShapeDtypeStruct((seq, hid), bf)] * 2 + [pltpu.VMEM(b.shape, bf) for b in (x_blk, w_blk, wo_blk)],
         scratch_shapes=[
             pltpu.VMEM((hid, w_loc), bf), pltpu.VMEM((2, t_loc, hid), bf), pltpu.VMEM((2, seq, t_loc), bf),
             pltpu.VMEM((ow, hid), bf), pltpu.VMEM((seq, hw), bf), pltpu.VMEM((seq, ow), bf),
@@ -466,43 +492,38 @@
             pltpu.VMEM((heads, seq, D), f32), pltpu.VMEM((heads, seq, D), f32),
             pltpu.VMEM((seq, hw), bf), pltpu.VMEM((seq, ow), bf),
             pltpu.VMEM((t_loc, w_loc), bf), pltpu.VMEM((ow, hid), bf), pltpu.VMEM((2 * t_loc, t_loc), f32),
-            pltpu.VMEM((t_loc, h_loc), bf), pltpu.VMEM((ow, h_loc), bf),
+            pltpu.VMEM((ow, h_loc), bf),
             pltpu.SemaphoreType.DMA((n_sem,)), pltpu.SemaphoreType.DMA((n_sem,)), pltpu.SemaphoreType.DMA((16,)),
         ],
-        compiler_params=pltpu.CompilerParams(collective_id=0, has_side_effects=True, vmem_limit_bytes=VMEM_LIMIT),
+        compiler_params=pltpu.CompilerParams(collective_id=0, has_side_effects=True, vmem_limit_bytes=STEP_LIMIT),
         name='mega_step',
     )(x_blk, w_blk, wo_blk, seg_blk, dy_blk)
 
 
 def copy_kernel(parts, *refs):
     n = len(parts)
-    ins, outs, bufs, sem_in, sem_out = refs[:n], refs[n:2 * n], refs[2 * n:3 * n], refs[3 * n], refs[3 * n + 1]
+    ins, outs, sem = refs[:n], refs[n:2 * n], refs[2 * n]
     moves = []
     for i in range(n):
         step = ins[i].shape[0] // parts[i]
         for j in range(parts[i]):
             rows = pl.ds(j * step, step)
-            load = pltpu.make_async_copy(ins[i].at[rows], bufs[i].at[rows], sem_in.at[len(moves)])
-            load.start()
-            moves.append((load, pltpu.make_async_copy(bufs[i].at[rows], outs[i].at[rows], sem_out.at[len(moves)])))
-    for load, store in moves:
-        load.wait()
-        store.start()
-    for _, store in moves:
-        store.wait()
+            move = pltpu.make_async_copy(ins[i].at[rows], outs[i].at[rows], sem.at[len(moves)])
+            move.start()
+            moves.append(move)
+    for move in moves:
+        move.wait()
 
 
 def copy_out(*arrays):
     parts = [a.shape[0] // 128 for a in arrays]
-    hbm = pl.BlockSpec(memory_space=pl.ANY)
-    shapes = [jax.ShapeDtypeStruct(a.shape, a.dtype) for a in arrays]
     return pl.pallas_call(
         functools.partial(copy_kernel, parts),
-        in_specs=[hbm] * len(arrays),
-        out_specs=[hbm] * len(arrays),
-        out_shape=shapes,
-        scratch_shapes=[pltpu.VMEM(a.shape, a.dtype) for a in arrays] + [pltpu.SemaphoreType.DMA((sum(parts),))] * 2,
-        compiler_params=pltpu.CompilerParams(vmem_limit_bytes=VMEM_LIMIT),
+        in_specs=[pl.BlockSpec(memory_space=pltpu.VMEM)] * len(arrays),
+        out_specs=[pl.BlockSpec(memory_space=pl.ANY)] * len(arrays),
+        out_shape=[jax.ShapeDtypeStruct(a.shape, a.dtype) for a in arrays],
+        scratch_shapes=[pltpu.SemaphoreType.DMA((sum(parts),))],
+        compiler_params=pltpu.CompilerParams(vmem_limit_bytes=1_000_000),
         name='copy_out',
     )(*arrays)
 

time: 215 us -> 213 us (level)
    pallas_call x2, Pallas kernels: 214 us -> 212 us  [the longest x1 210 us: step_all(): pl.pallas_call(step_kernel, in_specs=[hbm] * 5, out_specs=[hbm] * 2 + [pl...]
where the time goes in v4:
time: 213 us
  Pallas kernels  212 us (100%)
    pallas_call x1, Pallas kernels, step_all(): pl.pallas_call(step_kernel, in_specs=[hbm] * 5, out_specs=[hbm] * 2 + [pl...  210 us

profile of v4, /device:TPU:0, one launch (start us, length us, event | category | flops | bytes accessed | tf_op | source)
XLA Modules:
  0.0 212.9 jit_solution(7999251091522346154)
XLA Ops:
  0.6 209.6 %mega_step.1 = (bf16[2048,2048]{1,0:T(8,128)(2,1)}, bf16[2048,2048]{1,0:T(8,128)(2,1)}, bf16[512,1024]{1,0:T(8,128)(2,1)S(1)}, bf16[512,3072]{1,0:T(8,128)(2,1)S(1)}, bf16[512,1024]{1,0:T(8,128)(2,1)S(1)}) custom-call(bf16[512,1024]{1,0:T(8,128)(2,1)} %x_ref.1, bf16[512,3072]{1,0:T(8,128)(2,1)} %w_ref.1, bf16[512,1024]{1,0:T(8,128)(2,1)} %wo_ref.1, ...), custom_call_target="tpu_custom_call" | custom-call | tf_op jit(solution)/shard_map/mega_step/pallas_call | solution.py:481
  210.3 2.4 %copy_out.1 = (bf16[512,1024]{1,0:T(8,128)(2,1)}, bf16[512,3072]{1,0:T(8,128)(2,1)}, bf16[512,1024]{1,0:T(8,128)(2,1)}) custom-call(bf16[512,1024]{1,0:T(8,128)(2,1)S(1)} %get-tuple-element.6.refs_0_, bf16[512,3072]{1,0:T(8,128)(2,1)S(1)} %get-tuple-element.7.refs_1_, bf16[512,1024]{1,0:T(8,128)(2,1)S(1)} %get-tuple-element.8.refs_2_), custom_call_target="tpu_custom_call" | custom-call | tf_op jit(solution)/shard_map/copy_out/pallas_call | solution.py:520

commit v5 on v4

--- a/solution.py
+++ b/solution.py
@@ -163,9 +163,9 @@
         send(WB + 8 + t, wslot(r_x, q), wslot(r_x, q), sib)
 
     barrier = pltpu.get_barrier_semaphore()
-    for i in range(1, 8):
-        pl.semaphore_signal(barrier, inc=1, device_id={'row': lax.rem(r + i, 4), 'col': lax.rem(y + i // 4, 2)}, device_id_type=MESH)
-    pl.semaphore_wait(barrier, 7)
+    for dev in (xn, yn, sib):
+        pl.semaphore_signal(barrier, inc=1, device_id=dev, device_id_type=MESH)
+    pl.semaphore_wait(barrier, 3)
 
     send_own(x_ref, xg, XB, 1, xn)
     send_own(x_ref, xg, XB, 2, yn)
@@ -174,8 +174,8 @@
     send_own(x_ref, xg, XB, 0, sib)
     for t in range(4):
         w_own(t, 0, x, sib)
-    for i, (rr, dev) in enumerate(((r_s, sib), (r_x, xn), (r_xs, {'row': r_xs}))):
-        send(SGB + i, seg_ref, seg_v.at[r], dev)
+    send(SGB, seg_ref, seg_v.at[r], sib)
+    send(SGB + 1, seg_ref, seg_v.at[r], xn)
 
     a = local(1, x_ref, tok.at[0, :, pl.ds(0, h_loc)])
     b = local(2, dy_ref, tok.at[1, :, pl.ds(0, h_loc)])
@@ -192,6 +192,8 @@
     for j in range(NC):
         forward(xg, XB, 1, ((4, yn), (3, sib)), j)
         forward(xg, XB, 2, ((5, sib),), j)
+    take(xg, XB, 5)
+    send(SGB + 2, seg_ref, seg_v.at[r], {'row': r_xs})
     for k in range(2):
         row_to = 2 * c + k
         src = wo_ref.at[pl.ds(k * ow, ow)]
@@ -224,7 +226,7 @@
         return local(i, g.at[pl.ds(mult(rr, t_loc), t_loc), cols], tok.at[s, :, cols])
 
     blocks = (r, r_s, r_x, r_xs)
-    for kind in (0, 3, 5, 6):
+    for kind in (0, 3, 6):
         take(xg, XB, kind)
     loads = [load_tok(xg, blocks[i], i) for i in range(2)]
     w_forward(1)

time: 213 us -> 212 us (level)
  no operation moved by 1% of the time
where the time goes in v5:
time: 212 us; the launch traced here: 211 us
  Pallas kernels  211 us (100%)
    pallas_call x1, Pallas kernels, step_all(): pl.pallas_call(step_kernel, in_specs=[hbm] * 5, out_specs=[hbm] * 2 + [pl...  208 us

profile of v5, /device:TPU:0, one launch (start us, length us, event | category | flops | bytes accessed | tf_op | source)
XLA Modules:
  0.0 211.3 jit_solution(1062968156199857399)
XLA Ops:
  0.6 208.1 %mega_step.1 = (bf16[2048,2048]{1,0:T(8,128)(2,1)}, bf16[2048,2048]{1,0:T(8,128)(2,1)}, bf16[512,1024]{1,0:T(8,128)(2,1)S(1)}, bf16[512,3072]{1,0:T(8,128)(2,1)S(1)}, bf16[512,1024]{1,0:T(8,128)(2,1)S(1)}) custom-call(bf16[512,1024]{1,0:T(8,128)(2,1)} %x_ref.1, bf16[512,3072]{1,0:T(8,128)(2,1)} %w_ref.1, bf16[512,1024]{1,0:T(8,128)(2,1)} %wo_ref.1, ...), custom_call_target="tpu_custom_call" | custom-call | tf_op jit(solution)/shard_map/mega_step/pallas_call | solution.py:483
  208.7 2.4 %copy_out.1 = (bf16[512,1024]{1,0:T(8,128)(2,1)}, bf16[512,3072]{1,0:T(8,128)(2,1)}, bf16[512,1024]{1,0:T(8,128)(2,1)}) custom-call(bf16[512,1024]{1,0:T(8,128)(2,1)S(1)} %get-tuple-element.6.refs_0_, bf16[512,3072]{1,0:T(8,128)(2,1)S(1)} %get-tuple-element.7.refs_1_, bf16[512,1024]{1,0:T(8,128)(2,1)S(1)} %get-tuple-element.8.refs_2_), custom_call_target="tpu_custom_call" | custom-call | tf_op jit(solution)/shard_map/copy_out/pallas_call | solution.py:522

commit v6 on v5

--- a/solution.py
+++ b/solution.py
@@ -426,6 +426,23 @@
     d_x(0, y, p_scr)
     d_w(3)
     d_x(1, y, p_scr)
+    late = started[-(3 + NJ):]
+    for cp in started[:-(3 + NJ)]:
+        cp.wait_send()
+    half = dwo_v.at[:, pl.ds(0, h_loc)]
+    for k in range(2):
+        @pl.when(jnp.logical_not((x == y) & (2 * c + k == r)))
+        def _():
+            copy(WOB + k, WOB + k, wo_ref.at[pl.ds(0, ow)], half, sib).wait_send()
+
+        @pl.when(jnp.logical_not(((y == k) & (row_to == r)) | ((y != k) & (x != y))))
+        def _():
+            copy(DWO + k, DWO + k, half, relay, sib).wait_send()
+
+    @pl.when(jnp.logical_not(near))
+    def _():
+        copy(DWF, DWF, half, relay, yn).wait_send()
+
     for j in range(NJ):
         recv(PX + j, px_recv.at[pl.ds(2 * bt * j, 2 * bt)])
         for q in range(2):
@@ -450,21 +467,8 @@
         @pl.when(jnp.logical_not(mine | far))
         def _():
             recv(DWO + k, piece)
-    for cp in started:
+    for cp in late:
         cp.wait_send()
-    half = dwo_v.at[:, pl.ds(0, h_loc)]
-    for k in range(2):
-        @pl.when(jnp.logical_not((x == y) & (2 * c + k == r)))
-        def _():
-            copy(WOB + k, WOB + k, wo_ref.at[pl.ds(0, ow)], half, sib).wait_send()
-
-        @pl.when(jnp.logical_not(((y == k) & (row_to == r)) | ((y != k) & (x != y))))
-        def _():
-            copy(DWO + k, DWO + k, half, relay, sib).wait_send()
-
-    @pl.when(jnp.logical_not(near))
-    def _():
-        copy(DWF, DWF, half, relay, yn).wait_send()
 
     @pl.when(near)
     def _():

time: 212 us -> 211 us (level)
  no operation moved by 1% of the time
where the time goes in v6:
time: 211 us
  Pallas kernels  210 us (100%)
    pallas_call x1, Pallas kernels, step_all(): pl.pallas_call(step_kernel, in_specs=[hbm] * 5, out_specs=[hbm] * 2 + [pl...  208 us

profile of v6, /device:TPU:0, one launch (start us, length us, event | category | flops | bytes accessed | tf_op | source)
XLA Modules:
  0.0 211.3 jit_solution(17392813520793620866)
XLA Ops:
  0.6 208.0 %mega_step.1 = (bf16[2048,2048]{1,0:T(8,128)(2,1)}, bf16[2048,2048]{1,0:T(8,128)(2,1)}, bf16[512,1024]{1,0:T(8,128)(2,1)S(1)}, bf16[512,3072]{1,0:T(8,128)(2,1)S(1)}, bf16[512,1024]{1,0:T(8,128)(2,1)S(1)}) custom-call(bf16[512,1024]{1,0:T(8,128)(2,1)} %x_ref.1, bf16[512,3072]{1,0:T(8,128)(2,1)} %w_ref.1, bf16[512,1024]{1,0:T(8,128)(2,1)} %wo_ref.1, ...), custom_call_target="tpu_custom_call" | custom-call | tf_op jit(solution)/shard_map/mega_step/pallas_call | solution.py:487
  208.6 2.4 %copy_out.1 = (bf16[512,1024]{1,0:T(8,128)(2,1)}, bf16[512,3072]{1,0:T(8,128)(2,1)}, bf16[512,1024]{1,0:T(8,128)(2,1)}) custom-call(bf16[512,1024]{1,0:T(8,128)(2,1)S(1)} %get-tuple-element.6.refs_0_, bf16[512,3072]{1,0:T(8,128)(2,1)S(1)} %get-tuple-element.7.refs_1_, bf16[512,1024]{1,0:T(8,128)(2,1)S(1)} %get-tuple-element.8.refs_2_), custom_call_target="tpu_custom_call" | custom-call | tf_op jit(solution)/shard_map/copy_out/pallas_call | solution.py:526

commit v7 on v6

--- a/solution.py
+++ b/solution.py
@@ -522,7 +522,7 @@
 
 
 def copy_out(*arrays):
-    parts = [a.shape[0] // 128 for a in arrays]
+    parts = [a.shape[0] // 512 for a in arrays]
     return pl.pallas_call(
         functools.partial(copy_kernel, parts),
         in_specs=[pl.BlockSpec(memory_space=pltpu.VMEM)] * len(arrays),

time: 211 us -> 211 us (level)
  no operation moved by 1% of the time
where the time goes in v7:
time: 211 us
  Pallas kernels  210 us (100%)
    pallas_call x1, Pallas kernels, step_all(): pl.pallas_call(step_kernel, in_specs=[hbm] * 5, out_specs=[hbm] * 2 + [pl...  208 us

profile of v7, /device:TPU:0, one launch (start us, length us, event | category | flops | bytes accessed | tf_op | source)
XLA Modules:
  0.0 211.2 jit_solution(11132637418038887896)
XLA Ops:
  0.6 208.0 %mega_step.1 = (bf16[2048,2048]{1,0:T(8,128)(2,1)}, bf16[2048,2048]{1,0:T(8,128)(2,1)}, bf16[512,1024]{1,0:T(8,128)(2,1)S(1)}, bf16[512,3072]{1,0:T(8,128)(2,1)S(1)}, bf16[512,1024]{1,0:T(8,128)(2,1)S(1)}) custom-call(bf16[512,1024]{1,0:T(8,128)(2,1)} %x_ref.1, bf16[512,3072]{1,0:T(8,128)(2,1)} %w_ref.1, bf16[512,1024]{1,0:T(8,128)(2,1)} %wo_ref.1, ...), custom_call_target="tpu_custom_call" | custom-call | tf_op jit(solution)/shard_map/mega_step/pallas_call | solution.py:487
  208.6 2.4 %copy_out.1 = (bf16[512,1024]{1,0:T(8,128)(2,1)}, bf16[512,3072]{1,0:T(8,128)(2,1)}, bf16[512,1024]{1,0:T(8,128)(2,1)}) custom-call(bf16[512,1024]{1,0:T(8,128)(2,1)S(1)} %get-tuple-element.6.refs_0_, bf16[512,3072]{1,0:T(8,128)(2,1)S(1)} %get-tuple-element.7.refs_1_, bf16[512,1024]{1,0:T(8,128)(2,1)S(1)} %get-tuple-element.8.refs_2_), custom_call_target="tpu_custom_call" | custom-call | tf_op jit(solution)/shard_map/copy_out/pallas_call | solution.py:526
